TPU v7x, 64 devices: a 2x2x8 block of a 4x4x8 slice. The times are simulated.
64 devices in a mesh: rep: 4 (over x, y), dp: 16 (over z, core).
Axes of the slice: x: 2, y: 2, z: 8, core: 2. Of those that a mesh axis runs over, the one named last changes fastest.
The devices are a block of a 4x4x8 slice.
Arguments:
- x: bfloat16 [64, 1024, 896], P(('rep', 'dp')), parts along dimension 0
- dy: bfloat16 [64, 1024, 896], P(('rep', 'dp')), parts along dimension 0
- w_gate: bfloat16 [2, 896, 2560], replicated
- w_up: bfloat16 [2, 896, 2560], replicated
- w_down: bfloat16 [2, 2560, 896], replicated
- m_w_gate: float32 [2, 896, 2560], P(None, 'dp')
- m_w_up: float32 [2, 896, 2560], P(None, 'dp')
- m_w_down: float32 [2, 2560, 896], P(None, 'dp')
- v_w_gate: float32 [2, 896, 2560], P(None, 'dp')
- v_w_up: float32 [2, 896, 2560], P(None, 'dp')
- v_w_down: float32 [2, 2560, 896], P(None, 'dp')
Outputs:
- output 1: bfloat16 [8, 896, 2560], P('rep'), parts along dimension 0
- output 2: bfloat16 [8, 896, 2560], P('rep'), parts along dimension 0
- output 3: bfloat16 [8, 2560, 896], P('rep'), parts along dimension 0
- output 4: float32 [8, 896, 2560], P('rep', 'dp'), parts along dimension 0
- output 5: float32 [8, 896, 2560], P('rep', 'dp'), parts along dimension 0
- output 6: float32 [8, 2560, 896], P('rep', 'dp'), parts along dimension 0
- output 7: float32 [8, 896, 2560], P('rep', 'dp'), parts along dimension 0
- output 8: float32 [8, 896, 2560], P('rep', 'dp'), parts along dimension 0
- output 9: float32 [8, 2560, 896], P('rep', 'dp'), parts along dimension 0
There are 4 independent parts. A program takes and returns all parts, laid end to end along the dimension named above; an argument that names none is the same for every part.
All inputs are finite; a program needn't handle non-finite values.
Results may differ from a plain program's by a relative error of at most 0.022.
Values are sent between devices in bfloat16 or wider.
A program may use at most 768 MiB of HBM per device.

v0:
```python
import jax
import jax.numpy as jnp
from jax import lax

NAMES = ("w_gate", "w_up", "w_down")


def matmul(a, w):
    return jnp.dot(a, w, preferred_element_type=jnp.float32).astype(jnp.bfloat16)


def normed(h):
    wide = h.astype(jnp.float32)
    scale = lax.rsqrt(jnp.mean(wide**2, -1, keepdims=True) + 1e-6)
    return (wide * scale).astype(jnp.bfloat16)


def layer(h, w):
    a = normed(h)
    gate = jnp.dot(a, w["w_gate"], preferred_element_type=jnp.float32)
    up = jnp.dot(a, w["w_up"], preferred_element_type=jnp.float32)
    return h + matmul((jax.nn.silu(gate) * up).astype(jnp.bfloat16), w["w_down"])


def adamw(w, m, v, g):
    m = 0.9 * m + 0.1 * g
    v = 0.95 * v + 0.05 * g * g
    step = m * lax.rsqrt(v + 1e-8) + 0.1 * w
    return (w - 0.02 * step).astype(jnp.bfloat16), m, v


def clipped(gradients, sum_of_squares, count):
    factor = jnp.minimum(1.0, 0.5 * lax.rsqrt(sum_of_squares / count + 1e-30))
    return [g * factor for g in gradients]


def stack(weights, h):
    for number in range(weights["w_gate"].shape[0]):
        h = layer(h, {name: w[number] for name, w in weights.items()})
    return h


def solution(mesh):
    groups = mesh.shape["rep"]

    def step(x, dy, *arrays):
        weights, m, v = (arrays[i : i + 3] for i in (0, 3, 6))
        x, dy = (t.reshape(groups, -1, *t.shape[1:]) for t in (x, dy))

        def of_a_group(x, dy):
            _, back = jax.vjp(lambda w: stack(w, x), dict(zip(NAMES, weights, strict=True)))
            by_weights = back(dy)[0]
            gradients = [by_weights[name].astype(jnp.float32) for name in NAMES]
            gradients = clipped(gradients, sum(jnp.sum(g * g) for g in gradients), sum(g.size for g in gradients))
            new = [adamw(w.astype(jnp.float32), m, v, g) for w, m, v, g in zip(weights, m, v, gradients, strict=True)]
            return tuple(one[which] for which in range(3) for one in new)

        return tuple(t.reshape(-1, *t.shape[2:]) for t in jax.vmap(of_a_group)(x, dy))

    return step
```

profile of v0, /device:TPU:21, one launch (start us, length us, event | category | flops | bytes accessed | tf_op | source)
XLA Modules:
  0.0 743.2 jit_solution(9127679844232465977)
XLA Ops:
  7.3 2.0 fusion.67
  9.3 3.8 copy
  13.1 7.5 %fusion.56 = f32[1024,2560]{1,0:T(8,128)S(1)} fusion(bf16[2,896,2560]{2,1,0:T(8,128)(2,1)} %param, bf16[1,1024,896]{2,1,0:T(8,128)(2,1)S(1)} %copy-done.4, f32[1024]{0:T(1024)S(1)} %add_rsqrt_fusion), kind=kOutput, calls=%fused_computation.67 | convolution fusion | flops 4700372992 | bytes 16912384 | tf_op jit(solution)/vmap(jvp())/dot_general | solution.py:20
  20.7 9.3 %fusion.54 = f32[1024,2560]{1,0:T(8,128)S(1)} fusion(bf16[2,896,2560]{2,1,0:T(8,128)(2,1)} %param.3, bf16[1,1024,896]{2,1,0:T(8,128)(2,1)S(1)} %copy-done.4, f32[1024]{0:T(1024)S(1)} %add_rsqrt_fusion), kind=kOutput, calls=%fused_computation.65 | convolution fusion | flops 4700372992 | bytes 16912384 | tf_op jit(solution)/vmap(jvp())/dot_general | solution.py:21
  30.0 3.8 copy-done.1
  33.8 3.3 fusion.35
  37.2 9.5 %fusion.71 = (f32[1024]{0:T(1024)S(1)}, bf16[1,1,1024,896]{2,3,1,0:T(8,128)(2,1)S(1)}) fusion(bf16[1024,2560]{1,0:T(8,128)(2,1)S(1)} %fusion.35, bf16[2,2560,896]{2,1,0:T(8,128)(2,1)} %param.4, bf16[1,1024,896]{1,2,0:T(8,128)(2,1)S(1)} %copy-done.8), kind=kOutput, calls=%fused_computation.85 | convolution fusion | flops 4702206976 | bytes 13504512 | tf_op jit(solution)/vmap(jvp())/dot_general | solution.py:9
  46.7 1.2 copy-done.10
  47.9 7.8 %fusion.45 = f32[1024,2560]{1,0:T(8,128)S(1)} fusion(bf16[2,896,2560]{2,1,0:T(8,128)(2,1)} %param, bf16[1,1,1024,896]{2,3,1,0:T(8,128)(2,1)S(1)} %get-tuple-element.10, f32[1024]{0:T(1024)S(1)} %bitcast.323), kind=kOutput, calls=%fused_computation.56 | convolution fusion | flops 4700372992 | bytes 16912384 | tf_op jit(solution)/vmap(jvp())/dot_general | solution.py:20
  55.8 11.3 %fusion.48 = f32[1024,2560]{1,0:T(8,128)S(1)} fusion(bf16[2,896,2560]{2,1,0:T(8,128)(2,1)} %param.3, bf16[1,1,1024,896]{2,3,1,0:T(8,128)(2,1)} %copy-done.10, f32[1024]{0:T(1024)S(1)} %bitcast.324), kind=kOutput, calls=%fused_computation.59 | convolution fusion | flops 4700372992 | bytes 16912384 | tf_op jit(solution)/vmap(jvp())/dot_general | solution.py:21
  67.1 3.8 copy-done.3
  70.9 9.9 %convolution_bitcast_fusion.1 = f32[1,2560,896]{2,1,0:T(8,128)} fusion(f32[1024,2560]{1,0:T(8,128)S(1)} %fusion.48, f32[1024,2560]{1,0:T(8,128)S(1)} %fusion.45, bf16[1,1024,896]{2,1,0:T(8,128)(2,1)} %param.5), kind=kOutput, calls=%fused_computation.43 | convolution fusion | flops 4713349120 | bytes 31981568 | tf_op jit(solution)/vmap(transpose(jvp()))/dot_general | solution.py:9
  80.9 4.0 copy.1
  84.9 8.6 %convolution_convert_fusion.1 = bf16[1024,2560]{1,0:T(8,128)(2,1)S(1)} fusion(bf16[2,2560,896]{2,1,0:T(8,128)(2,1)} %param.4, bf16[1,1024,896]{2,1,0:T(8,128)(2,1)} %param.5), kind=kOutput, calls=%fused_computation.46 | convolution fusion | flops 4700241920 | bytes 11665408 | tf_op jit(solution)/vmap(transpose(jvp()))/dot_general | solution.py:9
  93.5 2.3 copy-done.7
  95.8 9.6 %fusion.6 = bf16[1024,2560]{1,0:T(8,128)(2,1)} fusion(f32[1024,2560]{1,0:T(8,128)S(1)} %bitcast.316, f32[1024,2560]{1,0:T(8,128)} %copy-done.3, bf16[1024,2560]{1,0:T(8,128)(2,1)S(1)} %convolution_convert_fusion.1), kind=kLoop, calls=%fused_computation.11 | loop fusion | flops 31457280 | bytes 31457280
  105.5 9.0 %fusion.24 = bf16[1024,896]{0,1:T(8,128)(2,1)S(1)} fusion(bf16[1024,2560]{1,0:T(8,128)(2,1)} %copy-done.7, f32[1024,2560]{1,0:T(8,128)S(1)} %bitcast.316, bf16[2,896,2560]{2,1,0:T(8,128)(2,1)} %param.3), kind=kOutput, calls=%fused_computation.34 | convolution fusion | flops 4713349120 | bytes 22151168 | tf_op jit(solution)/vmap(transpose(jvp()))/dot_general | solution.py:21
  114.5 9.1 %fusion.73 = (f32[1024]{0:T(1024)S(1)}, bf16[1024,896]{0,1:T(8,128)(2,1)S(1)}) fusion(bf16[1,1,1024,896]{2,3,1,0:T(8,128)(2,1)S(1)} %copy-done.11, bf16[1024,896]{0,1:T(8,128)(2,1)S(1)} %fusion.24, bf16[1024,2560]{1,0:T(8,128)(2,1)} %fusion.6, bf16[2,896,2560]{2,1,0:T(8,128)(2,1)} %param), kind=kOutput, calls=%fused_computation.87 | convolution fusion | flops 4702206976 | bytes 15339520 | tf_op jit(solution)/vmap(transpose(jvp()))/dot_general | solution.py:20
  123.7 1.3 fusion.77
  125.0 1.3 copy-done.13
  126.3 10.5 %convolution_bitcast_fusion = f32[1,2560,896]{2,1,0:T(8,128)} fusion(bf16[1024,2560]{1,0:T(8,128)(2,1)} %copy-done.6, bf16[1024,896]{0,1:T(8,128)(2,1)S(1)} %fusion.77), kind=kOutput, calls=%fused_computation.42 | convolution fusion | flops 4697620480 | bytes 16252928 | tf_op jit(solution)/vmap(transpose(jvp()))/dot_general | solution.py:9
  136.9 1.4 copy-done.12
  138.3 14.1 %fusion.26 = f32[1,896,2560]{2,1,0:T(8,128)} fusion(bf16[1024,2560]{1,0:T(8,128)(2,1)} %copy-done.7, f32[1024,2560]{1,0:T(8,128)} %copy-done.2, bf16[1,1,1024,896]{2,3,1,0:T(8,128)(2,1)S(1)} %copy-done.12, f32[1024]{0:T(1024)S(1)} %bitcast.326), kind=kOutput, calls=%fused_computation.39 | convolution fusion | flops 4716101632 | bytes 26742784 | tf_op jit(solution)/vmap(transpose(jvp()))/dot_general | solution.py:21
  152.5 8.8 %convolution_convert_fusion = bf16[1024,2560]{1,0:T(8,128)(2,1)S(1)} fusion(bf16[1024,896]{0,1:T(8,128)(2,1)} %copy-done.13, bf16[2,2560,896]{2,1,0:T(8,128)(2,1)} %param.4), kind=kOutput, calls=%fused_computation.45 | convolution fusion | flops 4700241920 | bytes 11665408 | tf_op jit(solution)/vmap(transpose(jvp()))/dot_general | solution.py:9
  161.4 2.3 copy-done.17
  163.7 12.8 %fusion.32 = f32[1,896,2560]{2,1,0:T(8,128)} fusion(bf16[1024,2560]{1,0:T(8,128)(2,1)S(1)} %convolution_convert_fusion, f32[1024,2560]{1,0:T(8,128)} %copy-done, bf16[1,1024,896]{1,2,0:T(8,128)(2,1)S(1)} %copy-done.9, f32[1024]{0:T(1024)S(1)} %add_rsqrt_fusion), kind=kOutput, calls=%fused_computation.41 | convolution fusion | flops 4716101632 | bytes 26742784 | tf_op jit(solution)/vmap(transpose(jvp()))/dot_general | solution.py:21
  176.6 11.6 %convolution_bitcast_fusion.2 = f32[1,896,2560]{2,1,0:T(8,128)} fusion(bf16[1024,2560]{1,0:T(8,128)(2,1)} %fusion.6, bf16[1,1,1024,896]{2,3,1,0:T(8,128)(2,1)} %copy-done.10, f32[1024]{0:T(1024)S(1)} %bitcast.327), kind=kOutput, calls=%fused_computation.44 | convolution fusion | flops 4700372992 | bytes 16257024 | tf_op jit(solution)/vmap(transpose(jvp()))/dot_general | solution.py:20
  188.4 13.9 %fusion.29 = f32[1,896,2560]{2,1,0:T(8,128)} fusion(f32[1024,2560]{1,0:T(8,128)} %copy-done, f32[1024,2560]{1,0:T(8,128)} %copy-done.1, bf16[1024,2560]{1,0:T(8,128)(2,1)} %copy-done.17, bf16[1,1024,896]{1,2,0:T(8,128)(2,1)S(1)} %copy-done.9, f32[1024]{0:T(1024)S(1)} %add_rsqrt_fusion), kind=kOutput, calls=%fused_computation.40 | convolution fusion | flops 4729208832 | bytes 37228544 | tf_op jit(solution)/vmap(transpose(jvp()))/dot_general | solution.py:20
  204.2 1.1 convert_bitcast_fusion.4
  205.3 16.8 %reduce-scatter.29.cloned.1.call-done = f32[1,160,896]{2,1,0:T(8,128)} async-done(((f32[1,2560,896]{2,1,0:T(8,128)}), f32[1,160,896]{2,1,0:T(8,128)}) %reduce-scatter.29.cloned.1.call-update) | async-done | bytes 573456
  222.1 1.1 convert_bitcast_fusion.3
  224.1 68.3 %reduce-scatter.23.cloned.1.call-done = f32[1,56,2560]{2,1,0:T(8,128)} async-done(((f32[1,896,2560]{2,1,0:T(8,128)}), f32[1,56,2560]{2,1,0:T(8,128)}) %reduce-scatter.23.cloned.1.call-update) | async-done | bytes 573456
  292.4 1.1 convert_bitcast_fusion.6
  293.5 69.7 %reduce-scatter.25.cloned.1.call-done = f32[1,56,2560]{2,1,0:T(8,128)} async-done(((f32[1,896,2560]{2,1,0:T(8,128)}), f32[1,56,2560]{2,1,0:T(8,128)}) %reduce-scatter.25.cloned.1.call-update) | async-done | bytes 573456
  365.1 68.7 %reduce-scatter.19.cloned.1.call-done = f32[1,56,2560]{2,1,0:T(8,128)} async-done(((f32[1,896,2560]{2,1,0:T(8,128)}), f32[1,56,2560]{2,1,0:T(8,128)}) %reduce-scatter.19.cloned.1.call-update) | async-done | bytes 573456
  433.9 1.1 convert_bitcast_fusion.8
  435.0 69.7 %reduce-scatter.21.cloned.1.call-done = f32[1,56,2560]{2,1,0:T(8,128)} async-done(((f32[1,896,2560]{2,1,0:T(8,128)}), f32[1,56,2560]{2,1,0:T(8,128)}) %reduce-scatter.21.cloned.1.call-update) | async-done | bytes 573456
  504.6 1.1 convert_bitcast_fusion.7
  508.6 27.5 %all-reduce.16 = f32[1]{0:T(128)} all-reduce(f32[1]{0:T(128)} %bitcast.50), channel_id=5, replica_groups=mesh['rep'=4,'dp'=16] {'dp'}, use_global_device_ids=true, to_apply=%region_3.4.clone | all-reduce | flops 1 | bytes 8 | tf_op jit(solution)/vmap()/reduce_sum | solution.py:54
  536.7 3.6 fusion.123
  540.5 4.0 fusion.125
  544.7 3.6 fusion.124
  548.4 50.1 %all-gather.14.cloned.1.call-done = bf16[1,2,2560,896]{3,2,1,0:T(8,128)(2,1)} async-done(((bf16[1,2,160,896]{3,2,1,0:T(8,128)(2,1)}), bf16[1,2,2560,896]{3,2,1,0:T(8,128)(2,1)}) %all-gather.14.cloned.1.call-update) | async-done | bytes 9175056 | tf_op jit(solution)/reshape | solution.py:58
  598.5 57.0 %all-gather.10.cloned.1.call-done = bf16[1,2,896,2560]{3,2,1,0:T(8,128)(2,1)} async-done(((bf16[1,2,56,2560]{3,2,1,0:T(8,128)(2,1)}), bf16[1,2,896,2560]{3,2,1,0:T(8,128)(2,1)}) %all-gather.10.cloned.1.call-update) | async-done | bytes 9175056 | tf_op jit(solution)/reshape | solution.py:58
  655.5 57.0 %all-gather.12.cloned.1.call-done = bf16[1,2,896,2560]{3,2,1,0:T(8,128)(2,1)} async-done(((bf16[1,2,56,2560]{3,2,1,0:T(8,128)(2,1)}), bf16[1,2,896,2560]{3,2,1,0:T(8,128)(2,1)}) %all-gather.12.cloned.1.call-update) | async-done | bytes 9175056 | tf_op jit(solution)/reshape | solution.py:58
  712.5 7.8 %copy.5 = bf16[2,896,2560]{2,1,0:T(8,128)(2,1)} copy(bf16[2,896,2560]{2,1,0:T(8,128)(2,1)} %bitcast.318) | data formatting | bytes 18350080
  720.3 7.8 %copy.6 = bf16[2,896,2560]{2,1,0:T(8,128)(2,1)} copy(bf16[2,896,2560]{2,1,0:T(8,128)(2,1)} %bitcast.319) | data formatting | bytes 18350080
  728.2 8.0 %copy.7 = bf16[2,2560,896]{2,1,0:T(8,128)(2,1)} copy(bf16[2,2560,896]{2,1,0:T(8,128)(2,1)} %bitcast.317) | data formatting | bytes 18350080
  (64 shorter events, 6.1 us)
Async XLA Ops:
  7.2 5.9 copy-start.4
  7.2 197.0 %reduce-scatter.27.cloned.1.call-start = ((), (), s32[]{:S(2)}) async-start(), calls=%async_computation.13 | async-start | bytes 9748480
  20.7 9.3 %copy-start = (f32[1024,2560]{1,0:T(8,128)}, f32[1024,2560]{1,0:T(8,128)S(1)}, u32[]{:S(2)}) copy-start(f32[1024,2560]{1,0:T(8,128)S(1)} %fusion.56) | copy-start | bytes 31457284
  30.0 3.8 copy-start.1
  33.8 3.4 copy-start.8
  37.1 9.5 %copy-start.6 = (bf16[1024,2560]{1,0:T(8,128)(2,1)}, bf16[1024,2560]{1,0:T(8,128)(2,1)S(1)}, u32[]{:S(2)}) copy-start(bf16[1024,2560]{1,0:T(8,128)(2,1)S(1)} %fusion.35) | copy-start | bytes 15728644
  46.7 1.2 copy-start.10
  55.8 11.3 %copy-start.2 = (f32[1024,2560]{1,0:T(8,128)}, f32[1024,2560]{1,0:T(8,128)S(1)}, u32[]{:S(2)}) copy-start(f32[1024,2560]{1,0:T(8,128)S(1)} %fusion.45) | copy-start | bytes 31457284
  67.0 3.8 copy-start.3
  80.8 141.3 %reduce-scatter.29.cloned.1.call-start = ((), (), s32[]{:S(2)}) async-start(), calls=%async_computation.14 | async-start | bytes 9748480
  80.9 14.9 %slice-start = ((s8[10485760]{0:T(1024)(128)(4,1)}), s8[2097152]{0:T(1024)(128)(4,1)S(1)}, s32[]{:S(2)}) async-start(s8[10485760]{0:T(1024)(128)(4,1)} %bitcast.315), calls=%async_computation.15 | async-start | bytes 4194304
  84.9 11.0 %slice-start.1 = ((s8[10485760]{0:T(1024)(128)(4,1)}), s8[4194304]{0:T(1024)(128)(4,1)S(1)}, s32[]{:S(2)}) async-start(s8[10485760]{0:T(1024)(128)(4,1)} %bitcast.315), calls=%async_computation.16 | async-start | bytes 8388608
  84.9 11.0 %slice-start.2 = ((s8[10485760]{0:T(1024)(128)(4,1)}), s8[4194304]{0:T(1024)(128)(4,1)S(1)}, s32[]{:S(2)}) async-start(s8[10485760]{0:T(1024)(128)(4,1)} %bitcast.315), calls=%async_computation.17 | async-start | bytes 8388608
  93.5 2.4 copy-start.7
  105.4 9.0 %copy-start.11 = (bf16[1,1,1024,896]{2,3,1,0:T(8,128)(2,1)S(1)}, bf16[1,1,1024,896]{2,3,1,0:T(8,128)(2,1)}, u32[]{:S(2)}) copy-start(bf16[1,1,1024,896]{2,3,1,0:T(8,128)(2,1)} %copy-done.10) | copy-start | bytes 5505028
  114.5 9.2 %copy-start.5 = (bf16[1,1024,896]{1,2,0:T(8,128)(2,1)S(1)}, bf16[1,1024,896]{1,2,0:T(8,128)(2,1)}, u32[]{:S(2)}) copy-start(bf16[1,1024,896]{1,2,0:T(8,128)(2,1)} %copy.1) | copy-start | bytes 5505028
  125.0 1.3 copy-start.13
  136.8 1.5 copy-start.12
  136.9 155.6 %reduce-scatter.23.cloned.1.call-start = ((), (), s32[]{:S(2)}) async-start(), calls=%async_computation.11 | async-start | bytes 9748480
  152.4 11.3 %copy-start.9 = (bf16[1,1024,896]{1,2,0:T(8,128)(2,1)S(1)}, bf16[1,1024,896]{1,2,0:T(8,128)(2,1)}, u32[]{:S(2)}) copy-start(bf16[1,1024,896]{1,2,0:T(8,128)(2,1)} %copy) | copy-start | bytes 5505028
  152.4 210.7 %reduce-scatter.25.cloned.1.call-start = ((), (), s32[]{:S(2)}) async-start(), calls=%async_computation.12 | async-start | bytes 9748480
  161.4 2.3 copy-start.17
  176.5 257.4 %reduce-scatter.19.cloned.1.call-start = ((), (), s32[]{:S(2)}) async-start(), calls=%async_computation.9 | async-start | bytes 9748480
  188.3 316.4 %reduce-scatter.21.cloned.1.call-start = ((), (), s32[]{:S(2)}) async-start(), calls=%async_computation.10 | async-start | bytes 9748480
  202.3 0.7 copy-start.16
  202.4 334.4 %copy-start.14 = (f32[2,160,896]{2,1,0:T(8,128)S(1)}, f32[2,160,896]{2,1,0:T(8,128)}, u32[]{:S(2)}) copy-start(f32[2,160,896]{2,1,0:T(8,128)} %param.10) | copy-start | bytes 3440644
  202.4 396.1 %all-gather.14.cloned.1.call-start = ((), (), s32[]{:S(2)}) async-start(), calls=%async_computation.8 | async-start | bytes 9748480 | tf_op jit(solution)/reshape | solution.py:58
  540.4 4.3 copy-start.15
  540.5 115.0 %all-gather.10.cloned.1.call-start = ((), (), s32[]{:S(2)}) async-start(), calls=%async_computation.6 | async-start | bytes 9748480 | tf_op jit(solution)/reshape | solution.py:58
  544.6 167.9 %all-gather.12.cloned.1.call-start = ((), (), s32[]{:S(2)}) async-start(), calls=%async_computation.7 | async-start | bytes 9748480 | tf_op jit(solution)/reshape | solution.py:58
Sparse Core Ops, SparseCore 0:
  81.0 70.7 reduce-scatter.26
  154.1 67.9 reduce-scatter.28
  224.5 67.8 reduce-scatter.22
  295.2 67.8 reduce-scatter.24
  366.0 67.8 reduce-scatter.18
  436.7 67.8 reduce-scatter.20
  540.6 57.8 all-gather.13
  600.7 54.7 all-gather.9
  657.7 54.7 all-gather.11
where the time goes:
time: 752 us; the launch traced here: 743 us
  waiting for transfers between devices  458 us (61%)
  matrix products  154 us (20%)
  local copies, waits for them, and re-layouts  48.8 us (6%)
  other arithmetic  36.9 us (5%)
  blocking collectives  27.5 us (4%)
  between operations  18 us (2%)
    unnamed x15, waiting for transfers between devices  294 us
    reshape x3, waiting for transfers between devices, step(): t.reshape(-1, *t.shape[2:])  164 us
    dot_general x5, matrix products, layer(): up = jnp.dot(a, w['w_up'], preferred_element_type=jnp.float32)  56.4 us
    dot_general x5, matrix products, layer(): gate = jnp.dot(a, w['w_gate'], preferred_element_type=jnp.float32)  50.1 us
    unnamed x47, local copies, waits for them, and re-layouts  48.2 us
    dot_general x5, matrix products, matmul(): jnp.dot(a, w, preferred_element_type=jnp.float32).astype(jnp.bfloat16)  47.3 us
    reduce_sum x1, blocking collectives, of_a_group(): jnp.sum(g * g)  27.5 us
  transfers between devices with their start and end apart: 9, of which 8 were waited for; matrix products, arithmetic and copies ran while one was open for 17% of the time, Pallas kernels for 0%

commit v1 on v0

v1 whole, which is shorter than its diff:
```python
import jax
import jax.numpy as jnp
from jax import lax
from jax.sharding import PartitionSpec as P

NAMES = ("w_gate", "w_up", "w_down")


def matmul(a, w):
    return jnp.dot(a, w, preferred_element_type=jnp.float32).astype(jnp.bfloat16)


def normed(h):
    wide = h.astype(jnp.float32)
    scale = lax.rsqrt(jnp.mean(wide**2, -1, keepdims=True) + 1e-6)
    return (wide * scale).astype(jnp.bfloat16)


def layer(h, w):
    a = normed(h)
    gate = jnp.dot(a, w["w_gate"], preferred_element_type=jnp.float32)
    up = jnp.dot(a, w["w_up"], preferred_element_type=jnp.float32)
    return h + matmul((jax.nn.silu(gate) * up).astype(jnp.bfloat16), w["w_down"])


def adamw(w, m, v, g):
    m = 0.9 * m + 0.1 * g
    v = 0.95 * v + 0.05 * g * g
    step = m * lax.rsqrt(v + 1e-8) + 0.1 * w
    return (w - 0.02 * step).astype(jnp.bfloat16), m, v


def stack(weights, h):
    for w in weights:
        h = layer(h, w)
    return h


def solution(mesh):
    def of_a_device(x, dy, *arrays):
        stacked, m, v = (arrays[i : i + 3] for i in (0, 3, 6))
        layers = stacked[0].shape[0]
        place = lax.axis_index("dp")
        weights = [{n: w[i] for n, w in zip(NAMES, stacked)} for i in range(layers)]
        _, back = jax.vjp(lambda w: stack(w, x[0]), weights)
        (terms,) = back(dy[0])
        sums = [
            {n: lax.psum_scatter(terms[i][n], "dp", scatter_dimension=0, tiled=True).astype(jnp.float32) for n in NAMES}
            for i in range(layers)
        ]
        square = lax.psum(sum(jnp.sum(g * g) for one in sums for g in one.values()), "dp")
        count = sum(w.size for w in stacked)
        factor = jnp.minimum(1.0, 0.5 * lax.rsqrt(square / count + 1e-30))
        new = []
        for n, w, m1, v1 in zip(NAMES, stacked, m, v):
            g = jnp.stack([one[n] for one in sums]) * factor
            rows = m1.shape[1]
            mine = lax.dynamic_slice_in_dim(w, place * rows, rows, 1)
            w1, m1, v1 = adamw(mine.astype(jnp.float32), m1, v1, g)
            new.append((lax.all_gather(w1, "dp", axis=1, tiled=True), m1, v1))
        return tuple(one[which] for which in range(3) for one in new)

    seq, whole, rows = P(("rep", "dp")), P(), P(None, "dp")
    return jax.shard_map(
        of_a_device,
        mesh=mesh,
        in_specs=(seq, seq) + (whole,) * 3 + (rows,) * 6,
        out_specs=(P("rep"),) * 3 + (P("rep", "dp"),) * 6,
        check_vma=False,
    )
```

time: 752 us -> 747 us (level)
  matrix products: 154 us -> 168 us
  local copies, waits for them, and re-layouts: 48.8 us -> 35.8 us
  other arithmetic: 36.9 us -> 27.5 us
    reduce_scatter x0 -> x6, waiting for transfers between devices: none -> 300 us  [of_a_device(): lax.psum_scatter(terms[i][n], 'dp', scatter_dimension=0, tiled=True)]
    unnamed x15 -> x9, waiting for transfers between devices: 294 us -> 0.48 us
    reshape x3 -> x0, waiting for transfers between devices: 164 us -> none  [step(): t.reshape(-1, *t.shape[2:])]
    all_gather x0 -> x3, waiting for transfers between devices: none -> 161 us  [of_a_device(): new.append((lax.all_gather(w1, 'dp', axis=1, tiled=True), m1, v1))]
    reduce_sum x1 -> x0, blocking collectives: 27.5 us -> none  [of_a_group(): jnp.sum(g * g)]
    psum x0 -> x1, blocking collectives: none -> 27.5 us  [of_a_device(): lax.psum(sum((jnp.sum(g * g) for one in sums for g in one.values())), 'dp')]
    unnamed x4 -> x3, other arithmetic: 14.3 us -> 0.01 us
    unnamed x47, local copies, waits for them, and re-layouts: 48.2 us -> 35.8 us
  transfers between devices with their start and end apart: 9 -> 9, of which waited for: 8 -> 9; matrix products, arithmetic and copies ran while one was open for 17% -> 10% of each run, Pallas kernels for 0% -> 0%
where the time goes in v1:
time: 747 us; the launch traced here: 740 us
  waiting for transfers between devices  462 us (62%)
  matrix products  168 us (22%)
  local copies, waits for them, and re-layouts  35.8 us (5%)
  other arithmetic  27.5 us (4%)
  blocking collectives  27.5 us (4%)
  between operations  19 us (3%)
    reduce_scatter x6, waiting for transfers between devices, of_a_device(): lax.psum_scatter(terms[i][n], 'dp', scatter_dimension=0, tiled=True)  300 us
    all_gather x3, waiting for transfers between devices, of_a_device(): new.append((lax.all_gather(w1, 'dp', axis=1, tiled=True), m1, v1))  161 us
    dot_general x5, matrix products, layer(): gate = jnp.dot(a, w['w_gate'], preferred_element_type=jnp.float32)  60 us
    dot_general x5, matrix products, layer(): up = jnp.dot(a, w['w_up'], preferred_element_type=jnp.float32)  58.8 us
    dot_general x5, matrix products, matmul(): jnp.dot(a, w, preferred_element_type=jnp.float32).astype(jnp.bfloat16)  49.4 us
    unnamed x47, local copies, waits for them, and re-layouts  35.8 us
    psum x1, blocking collectives, of_a_device(): lax.psum(sum((jnp.sum(g * g) for one in sums for g in one.values())), 'dp')  27.5 us
  transfers between devices with their start and end apart: 9, of which 9 were waited for; matrix products, arithmetic and copies ran while one was open for 10% of the time, Pallas kernels for 0%

profile of v1, /device:TPU:21, one launch (start us, length us, event | category | flops | bytes accessed | tf_op | source)
XLA Modules:
  0.0 740.2 jit_solution(11410170388465710478)
XLA Ops:
  7.3 2.9 copy.20
  10.6 3.8 copy.21
  14.4 10.0 %convolution_convert_fusion.1 = bf16[1024,2560]{1,0:T(8,128)(2,1)} fusion(bf16[2,2560,896]{2,1,0:T(8,128)(2,1)} %param.15, bf16[1,1024,896]{2,1,0:T(8,128)(2,1)} %param.12), kind=kOutput, calls=%fused_computation.27 | convolution fusion | flops 4700241920 | bytes 11665408 | tf_op jit(solution)/shard_map/transpose(jvp())/dot_general | solution.py:10
  24.5 10.9 %fusion.32 = f32[1024,2560]{1,0:T(8,128)} fusion(bf16[2,896,2560]{2,1,0:T(8,128)(2,1)} %param.13, bf16[1,1024,896]{2,1,0:T(8,128)(2,1)S(1)} %copy-done.1, f32[1024]{0:T(1024)S(1)} %add_rsqrt_fusion), kind=kOutput, calls=%fused_computation.48 | convolution fusion | flops 4700372992 | bytes 16912384 | tf_op jit(solution)/shard_map/jvp()/dot_general | solution.py:21
  35.3 13.4 %multiply_convert_fusion.1 = (bf16[1024,2560]{1,0:T(8,128)(2,1)}, f32[1024,2560]{1,0:T(8,128)}) fusion(f32[1024,2560]{1,0:T(8,128)} %fusion.32, bf16[2,896,2560]{2,1,0:T(8,128)(2,1)} %param.14, bf16[1,1024,896]{2,1,0:T(8,128)(2,1)S(1)} %copy-done.1, f32[1024]{0:T(1024)S(1)} %add_rsqrt_fusion), kind=kOutput, calls=%fused_computation.17 | convolution fusion | flops 4716101632 | bytes 32641024 | tf_op jit(solution)/shard_map/jvp()/dot_general | solution.py:22
  48.8 7.7 %fusion.47 = (f32[1024]{0:T(1024)S(1)}, bf16[1024,896]{0,1:T(8,128)(2,1)S(1)}) fusion(bf16[1024,2560]{1,0:T(8,128)(2,1)} %get-tuple-element.18, bf16[2,2560,896]{2,1,0:T(8,128)(2,1)S(1)} %bitcast.75, bf16[1,1024,896]{1,2,0:T(8,128)(2,1)S(1)} %copy.20), kind=kOutput, calls=%fused_computation.66 | convolution fusion | flops 4702206976 | bytes 13504512 | tf_op jit(solution)/shard_map/jvp()/dot_general | solution.py:10
  56.6 11.2 %fusion.19 = f32[1024,2560]{1,0:T(8,128)} fusion(bf16[2,896,2560]{2,1,0:T(8,128)(2,1)} %param.14, bf16[1024,896]{0,1:T(8,128)(2,1)S(1)} %get-tuple-element.21, f32[1024]{0:T(1024)S(1)} %fusion.85), kind=kOutput, calls=%fused_computation.35 | convolution fusion | flops 4700372992 | bytes 16912384 | tf_op jit(solution)/shard_map/jvp()/dot_general | solution.py:22
  67.8 17.4 %fusion.2 = (bf16[1024,2560]{1,0:T(8,128)(2,1)}, f32[1024,2560]{1,0:T(8,128)}) fusion(f32[1024,2560]{1,0:T(8,128)} %fusion.19, bf16[1024,2560]{1,0:T(8,128)(2,1)} %convolution_convert_fusion.1, bf16[2,896,2560]{2,1,0:T(8,128)(2,1)} %param.13, bf16[1024,896]{0,1:T(8,128)(2,1)S(1)} %get-tuple-element.21, f32[1024]{0:T(1024)S(1)} %fusion.85), kind=kOutput, calls=%fused_computation.8 | convolution fusion | flops 4731830272 | bytes 37883904 | tf_op jit(solution)/shard_map/jvp()/dot_general | solution.py:21
  85.2 11.8 %fusion.12 = bf16[1024,896]{0,1:T(8,128)(2,1)} fusion(bf16[1024,2560]{1,0:T(8,128)(2,1)} %convolution_convert_fusion.1, bf16[2,896,2560]{2,1,0:T(8,128)(2,1)S(1)} %bitcast.77, f32[1024,2560]{1,0:T(8,128)} %get-tuple-element.23), kind=kOutput, calls=%fused_computation.21 | convolution fusion | flops 4713349120 | bytes 22151168 | tf_op jit(solution)/shard_map/transpose(jvp())/dot_general | solution.py:22
  97.0 9.6 %fusion.49 = (f32[1024]{0:T(1024)S(1)}, bf16[1024,896]{0,1:T(8,128)(2,1)S(1)}) fusion(bf16[1024,896]{0,1:T(8,128)(2,1)S(1)} %get-tuple-element.21, bf16[1024,896]{0,1:T(8,128)(2,1)} %fusion.12, bf16[1024,2560]{1,0:T(8,128)(2,1)} %get-tuple-element.22, bf16[2,896,2560]{2,1,0:T(8,128)(2,1)} %param.13), kind=kOutput, calls=%fused_computation.68 | convolution fusion | flops 4702206976 | bytes 15339520 | tf_op jit(solution)/shard_map/transpose(jvp())/dot_general | solution.py:21
  106.7 1.4 fusion.51
  108.1 1.2 copy-done.5
  109.3 10.3 %convolution_convert_fusion = bf16[1024,2560]{1,0:T(8,128)(2,1)} fusion(bf16[1024,896]{0,1:T(8,128)(2,1)S(1)} %fusion.51, bf16[2,2560,896]{2,1,0:T(8,128)(2,1)} %param.15), kind=kOutput, calls=%fused_computation.26 | convolution fusion | flops 4700241920 | bytes 11665408 | tf_op jit(solution)/shard_map/transpose(jvp())/dot_general | solution.py:10
  119.7 9.7 %fusion.17 = bf16[896,2560]{1,0:T(8,128)(2,1)} fusion(bf16[1024,2560]{1,0:T(8,128)(2,1)} %convolution_convert_fusion, f32[1024,2560]{1,0:T(8,128)S(1)} %bitcast.79, bf16[1,1024,896]{1,2,0:T(8,128)(2,1)S(1)} %copy.20, f32[1024]{0:T(1024)S(1)} %add_rsqrt_fusion), kind=kOutput, calls=%fused_computation.31 | convolution fusion | flops 4718395392 | bytes 22155264 | tf_op jit(solution)/shard_map/transpose(jvp())/dot_general | solution.py:22
  129.5 13.1 %fusion.14 = bf16[896,2560]{1,0:T(8,128)(2,1)} fusion(f32[1024,2560]{1,0:T(8,128)} %fusion.32, f32[1024,2560]{1,0:T(8,128)} %get-tuple-element.19, bf16[1024,2560]{1,0:T(8,128)(2,1)} %convolution_convert_fusion, bf16[1,1024,896]{1,2,0:T(8,128)(2,1)S(1)} %copy.20, f32[1024]{0:T(1024)S(1)} %add_rsqrt_fusion), kind=kOutput, calls=%fused_computation.30 | convolution fusion | flops 4731502592 | bytes 32641024 | tf_op jit(solution)/shard_map/transpose(jvp())/dot_general | solution.py:21
  142.7 1.4 copy-done.6
  144.1 9.7 %convolution_convert_fusion.4 = bf16[2560,896]{1,0:T(8,128)(2,1)} fusion(bf16[1024,2560]{1,0:T(8,128)(2,1)} %get-tuple-element.18, bf16[1024,896]{0,1:T(8,128)(2,1)S(1)} %copy-done.6), kind=kOutput, calls=%fused_computation.33 | convolution fusion | flops 4699914240 | bytes 11665408 | tf_op jit(solution)/shard_map/transpose(jvp())/dot_general | solution.py:10
  153.9 1.4 copy-done.4
  155.3 9.1 %convolution_convert_fusion.2 = bf16[896,2560]{1,0:T(8,128)(2,1)} fusion(bf16[1024,2560]{1,0:T(8,128)(2,1)} %get-tuple-element.22, bf16[1024,896]{0,1:T(8,128)(2,1)S(1)} %copy-done.4, f32[1024]{0:T(1024)S(1)} %fusion.85), kind=kOutput, calls=%fused_computation.28 | convolution fusion | flops 4700372992 | bytes 11669504 | tf_op jit(solution)/shard_map/transpose(jvp())/dot_general | solution.py:21
  164.6 12.7 %fusion.13 = bf16[896,2560]{1,0:T(8,128)(2,1)} fusion(bf16[1024,2560]{1,0:T(8,128)(2,1)} %convolution_convert_fusion.1, bf16[1024,896]{0,1:T(8,128)(2,1)S(1)} %copy-done.4, f32[1024]{0:T(1024)S(1)} %fusion.85, f32[1024,2560]{1,0:T(8,128)} %get-tuple-element.23), kind=kOutput, calls=%fused_computation.29 | convolution fusion | flops 4718395392 | bytes 22155264 | tf_op jit(solution)/shard_map/transpose(jvp())/dot_general | solution.py:22
  177.4 1.4 copy-done.2
  178.8 11.6 %convolution_convert_fusion.3 = bf16[2560,896]{1,0:T(8,128)(2,1)} fusion(f32[1024,2560]{1,0:T(8,128)} %fusion.19, bf16[1,1024,896]{2,1,0:T(8,128)(2,1)S(1)} %copy-done.2, f32[1024,2560]{1,0:T(8,128)} %get-tuple-element.23), kind=kOutput, calls=%fused_computation.32 | convolution fusion | flops 4715642880 | bytes 27394048 | tf_op jit(solution)/shard_map/transpose(jvp())/dot_general | solution.py:10
  190.5 1.3 reduce-scatter.11.cloned.1.call-done
  191.8 1.7 fusion.81
  193.5 60.1 %reduce-scatter.7.cloned.1.call-done = bf16[56,2560]{1,0:T(8,128)(2,1)} async-done(((bf16[896,2560]{1,0:T(8,128)(2,1)}), bf16[56,2560]{1,0:T(8,128)(2,1)}) %reduce-scatter.7.cloned.1.call-update) | async-done | bytes 286736 | tf_op jit(solution)/shard_map/reduce_scatter | solution.py:48
  253.6 1.7 fusion.79
  256.6 58.8 %reduce-scatter.13.cloned.1.call-done = bf16[160,896]{1,0:T(8,128)(2,1)} async-done(((bf16[2560,896]{1,0:T(8,128)(2,1)}), bf16[160,896]{1,0:T(8,128)(2,1)}) %reduce-scatter.13.cloned.1.call-update) | async-done | bytes 286736 | tf_op jit(solution)/shard_map/reduce_scatter | solution.py:48
  315.4 1.7 fusion.82
  317.8 59.9 %reduce-scatter.9.cloned.1.call-done = bf16[56,2560]{1,0:T(8,128)(2,1)} async-done(((bf16[896,2560]{1,0:T(8,128)(2,1)}), bf16[56,2560]{1,0:T(8,128)(2,1)}) %reduce-scatter.9.cloned.1.call-update) | async-done | bytes 286736 | tf_op jit(solution)/shard_map/reduce_scatter | solution.py:48
  377.7 1.7 fusion.80
  380.1 59.9 %reduce-scatter.15.cloned.1.call-done = bf16[56,2560]{1,0:T(8,128)(2,1)} async-done(((bf16[896,2560]{1,0:T(8,128)(2,1)}), bf16[56,2560]{1,0:T(8,128)(2,1)}) %reduce-scatter.15.cloned.1.call-update) | async-done | bytes 286736 | tf_op jit(solution)/shard_map/reduce_scatter | solution.py:48
  440.0 1.7 fusion.83
  442.3 59.9 %reduce-scatter.17.cloned.1.call-done = bf16[160,896]{1,0:T(8,128)(2,1)} async-done(((bf16[2560,896]{1,0:T(8,128)(2,1)}), bf16[160,896]{1,0:T(8,128)(2,1)}) %reduce-scatter.17.cloned.1.call-update) | async-done | bytes 286736 | tf_op jit(solution)/shard_map/reduce_scatter | solution.py:48
  502.2 1.7 fusion.84
  504.6 27.5 %psum.7 = f32[]{:T(128)} all-reduce(f32[]{:T(128)S(6)} %add.116), channel_id=1, replica_groups=mesh['rep'=4,'dp'=16] {'dp'}, use_global_device_ids=true, to_apply=%region_15.16 | all-reduce | flops 1 | bytes 8 | tf_op jit(solution)/shard_map/psum | solution.py:51
  532.7 1.0 convert_bitcast_fusion
  533.7 1.0 convert_bitcast_fusion.2
  534.8 3.0 fusion.73
  538.0 1.0 convert_bitcast_fusion.1
  540.0 3.5 fusion.70
  543.6 1.0 convert_bitcast_fusion.4
  545.6 3.0 fusion.67
  548.6 47.1 %all-gather.8.cloned.1.call-done = bf16[2,2560,896]{2,1,0:T(8,128)(2,1)} async-done(((bf16[2,160,896]{2,1,0:T(8,128)(2,1)}), bf16[2,2560,896]{2,1,0:T(8,128)(2,1)}) %all-gather.8.cloned.1.call-update) | async-done | bytes 9175056 | tf_op jit(solution)/shard_map/all_gather | solution.py:60
  595.8 57.0 %all-gather.6.cloned.1.call-done = bf16[2,896,2560]{2,1,0:T(8,128)(2,1)} async-done(((bf16[2,56,2560]{2,1,0:T(8,128)(2,1)}), bf16[2,896,2560]{2,1,0:T(8,128)(2,1)}) %all-gather.6.cloned.1.call-update) | async-done | bytes 9175056 | tf_op jit(solution)/shard_map/all_gather | solution.py:60
  652.8 57.0 %all-gather.4.cloned.1.call-done = bf16[2,896,2560]{2,1,0:T(8,128)(2,1)} async-done(((bf16[2,56,2560]{2,1,0:T(8,128)(2,1)}), bf16[2,896,2560]{2,1,0:T(8,128)(2,1)}) %all-gather.4.cloned.1.call-update) | async-done | bytes 9175056 | tf_op jit(solution)/shard_map/all_gather | solution.py:60
  709.8 7.8 %copy.25 = bf16[2,896,2560]{2,1,0:T(8,128)(2,1)} copy(bf16[2,896,2560]{2,1,0:T(8,128)(2,1)} %all-gather.4.cloned.1.call-done) | data formatting | bytes 18350080
  717.6 7.8 %copy.26 = bf16[2,896,2560]{2,1,0:T(8,128)(2,1)} copy(bf16[2,896,2560]{2,1,0:T(8,128)(2,1)} %all-gather.6.cloned.1.call-done) | data formatting | bytes 18350080
  725.5 8.0 %copy.27 = bf16[2,2560,896]{2,1,0:T(8,128)(2,1)} copy(bf16[2,2560,896]{2,1,0:T(8,128)(2,1)} %all-gather.8.cloned.1.call-done) | data formatting | bytes 18350080
  (65 shorter events, 3.6 us)
Async XLA Ops:
  7.2 184.6 %reduce-scatter.11.cloned.1.call-start = ((), (), s32[]{:S(2)}) async-start(), calls=%async_computation.8 | async-start | bytes 4874240 | tf_op jit(solution)/shard_map/reduce_scatter | solution.py:48
  14.4 10.0 %copy-start.1 = (bf16[1,1024,896]{2,1,0:T(8,128)(2,1)S(1)}, bf16[1,1024,896]{2,1,0:T(8,128)(2,1)}, u32[]{:S(2)}) copy-start(bf16[1,1024,896]{2,1,0:T(8,128)(2,1)} %param.11) | copy-start | bytes 5505028
  24.5 24.3 %slice-start = ((s8[9175040]{0:T(1024)(128)(4,1)}), s8[4194304]{0:T(1024)(128)(4,1)S(1)}, s32[]{:S(2)}) async-start(s8[9175040]{0:T(1024)(128)(4,1)} %bitcast.74), calls=%async_computation.15 | async-start | bytes 8388608
  35.3 13.5 %slice-start.1 = ((s8[9175040]{0:T(1024)(128)(4,1)}), s8[4194304]{0:T(1024)(128)(4,1)S(1)}, s32[]{:S(2)}) async-start(s8[9175040]{0:T(1024)(128)(4,1)} %bitcast.74), calls=%async_computation.16 | async-start | bytes 8388608
  35.3 13.5 %slice-start.2 = ((s8[9175040]{0:T(1024)(128)(4,1)}), s8[786432]{0:T(1024)(128)(4,1)S(1)}, s32[]{:S(2)}) async-start(s8[9175040]{0:T(1024)(128)(4,1)} %bitcast.74), calls=%async_computation.17 | async-start | bytes 1572864
  56.5 50.1 %copy-start.3 = (bf16[1024,896]{0,1:T(8,128)(2,1)}, bf16[1024,896]{0,1:T(8,128)(2,1)S(1)}, u32[]{:S(2)}) copy-start(bf16[1024,896]{0,1:T(8,128)(2,1)S(1)} %get-tuple-element.21) | copy-start | bytes 5505028
  56.6 28.6 %slice-start.3 = ((s8[9175040]{0:T(1024)(128)(4,1)}), s8[4194304]{0:T(1024)(128)(4,1)S(1)}, s32[]{:S(2)}) async-start(s8[9175040]{0:T(1024)(128)(4,1)} %bitcast.76), calls=%async_computation.18 | async-start | bytes 8388608
  67.8 17.4 %slice-start.4 = ((s8[9175040]{0:T(1024)(128)(4,1)}), s8[4194304]{0:T(1024)(128)(4,1)S(1)}, s32[]{:S(2)}) async-start(s8[9175040]{0:T(1024)(128)(4,1)} %bitcast.76), calls=%async_computation.19 | async-start | bytes 8388608
  67.8 17.4 %slice-start.5 = ((s8[9175040]{0:T(1024)(128)(4,1)}), s8[786432]{0:T(1024)(128)(4,1)S(1)}, s32[]{:S(2)}) async-start(s8[9175040]{0:T(1024)(128)(4,1)} %bitcast.76), calls=%async_computation.20 | async-start | bytes 1572864
  97.0 9.6 %copy-start = (bf16[1,1024,896]{1,2,0:T(8,128)(2,1)S(1)}, bf16[1,1024,896]{1,2,0:T(8,128)(2,1)}, u32[]{:S(2)}) copy-start(bf16[1,1024,896]{1,2,0:T(8,128)(2,1)} %copy.21) | copy-start | bytes 5505028
  106.7 13.0 %slice-start.6 = ((s8[10485760]{0:T(1024)(128)(4,1)}), s8[2097152]{0:T(1024)(128)(4,1)S(1)}, s32[]{:S(2)}) async-start(s8[10485760]{0:T(1024)(128)(4,1)} %bitcast.78), calls=%async_computation.21 | async-start | bytes 4194304
  108.0 1.2 copy-start.5
  109.3 10.4 %slice-start.7 = ((s8[10485760]{0:T(1024)(128)(4,1)}), s8[4194304]{0:T(1024)(128)(4,1)S(1)}, s32[]{:S(2)}) async-start(s8[10485760]{0:T(1024)(128)(4,1)} %bitcast.78), calls=%async_computation.22 | async-start | bytes 8388608
  109.3 10.4 %slice-start.8 = ((s8[10485760]{0:T(1024)(128)(4,1)}), s8[4194304]{0:T(1024)(128)(4,1)S(1)}, s32[]{:S(2)}) async-start(s8[10485760]{0:T(1024)(128)(4,1)} %bitcast.78), calls=%async_computation.23 | async-start | bytes 8388608
  129.4 124.2 %reduce-scatter.7.cloned.1.call-start = ((), (), s32[]{:S(2)}) async-start(), calls=%async_computation.6 | async-start | bytes 4874240 | tf_op jit(solution)/shard_map/reduce_scatter | solution.py:48
  142.6 1.5 copy-start.6
  142.6 172.8 %reduce-scatter.13.cloned.1.call-start = ((), (), s32[]{:S(2)}) async-start(), calls=%async_computation.9 | async-start | bytes 4874240 | tf_op jit(solution)/shard_map/reduce_scatter | solution.py:48
  153.8 1.5 copy-start.4
  153.9 223.8 %reduce-scatter.9.cloned.1.call-start = ((), (), s32[]{:S(2)}) async-start(), calls=%async_computation.7 | async-start | bytes 4874240 | tf_op jit(solution)/shard_map/reduce_scatter | solution.py:48
  164.5 275.5 %reduce-scatter.15.cloned.1.call-start = ((), (), s32[]{:S(2)}) async-start(), calls=%async_computation.10 | async-start | bytes 4874240 | tf_op jit(solution)/shard_map/reduce_scatter | solution.py:48
  177.3 1.5 copy-start.2
  177.4 324.9 %reduce-scatter.17.cloned.1.call-start = ((), (), s32[]{:S(2)}) async-start(), calls=%async_computation.11 | async-start | bytes 4874240 | tf_op jit(solution)/shard_map/reduce_scatter | solution.py:48
  190.4 344.4 %copy-start.7 = (f32[2,160,896]{2,1,0:T(8,128)S(1)}, f32[2,160,896]{2,1,0:T(8,128)}, u32[]{:S(2)}) copy-start(f32[2,160,896]{2,1,0:T(8,128)} %param.21) | copy-start | bytes 3440644
  190.4 344.4 %copy-start.8 = (f32[2,160,896]{2,1,0:T(8,128)S(1)}, f32[2,160,896]{2,1,0:T(8,128)}, u32[]{:S(2)}) copy-start(f32[2,160,896]{2,1,0:T(8,128)} %param.18) | copy-start | bytes 3440644
  190.4 405.3 %all-gather.8.cloned.1.call-start = ((), (), s32[]{:S(2)}) async-start(), calls=%async_computation.14 | async-start | bytes 9748480 | tf_op jit(solution)/shard_map/all_gather | solution.py:60
  534.8 5.2 copy-start.9
  537.9 114.9 %all-gather.6.cloned.1.call-start = ((), (), s32[]{:S(2)}) async-start(), calls=%async_computation.13 | async-start | bytes 9748480 | tf_op jit(solution)/shard_map/all_gather | solution.py:60
  540.0 5.6 copy-start.10
  540.0 5.6 copy-start.11
  543.5 166.2 %all-gather.4.cloned.1.call-start = ((), (), s32[]{:S(2)}) async-start(), calls=%async_computation.12 | async-start | bytes 9748480 | tf_op jit(solution)/shard_map/all_gather | solution.py:60
Sparse Core Ops, SparseCore 0:
  129.5 62.1 reduce-scatter.10
  194.1 59.4 reduce-scatter.6
  256.0 59.4 reduce-scatter.12
  318.2 59.4 reduce-scatter.8
  380.5 59.4 reduce-scatter.14
  442.7 59.4 reduce-scatter.16
  538.0 57.7 all-gather.7
  598.0 54.7 all-gather.5
  655.0 54.7 all-gather.3

commit v2 on v1

v2 whole, which is shorter than its diff:
```python
import functools

import jax
import jax.numpy as jnp
from jax import lax
from jax.experimental import pallas as pl
from jax.experimental.pallas import tpu as pltpu
from jax.sharding import PartitionSpec as P

MESH = pl.DeviceIdType.MESH
BF, F32 = jnp.bfloat16, jnp.float32
LANES = 128
TILE = 512
QUARTERS = TILE // LANES
ROWS = 512
LAG = 2
LAG_PARTNER = 1
RING_GRAD, RING_SUM, RING_PARTNER = 16, 10, 4
VMEM_LIMIT = 66_000_000


def nn(a, b):
    return lax.dot_general(a, b, (((1,), (0,)), ((), ())), preferred_element_type=F32)


def nt(a, b):
    return lax.dot_general(a, b, (((1,), (1,)), ((), ())), preferred_element_type=F32)


def tn(a, b):
    return lax.dot_general(a, b, (((0,), (0,)), ((), ())), preferred_element_type=F32)


def normed(h):
    wide = h.astype(F32)
    scale = lax.rsqrt(jnp.mean(wide * wide, -1, keepdims=True) + 1e-6)
    return (wide * scale).astype(BF)


def sigmoid(x):
    return 1.0 / (1.0 + jnp.exp(-x))


def forward_kernel(tiles, x_ref, wg_ref, wu_ref, wd_ref, a_ref, at_ref, h_ref, b_ref, bt_ref, acc):
    t = pl.program_id(0)

    @pl.when(t == 0)
    def _():
        a = normed(x_ref[...])
        a_ref[...] = a
        at_ref[...] = a.T
        acc[...] = jnp.zeros_like(acc)

    for r in range(0, x_ref.shape[0], ROWS):
        a = a_ref[r : r + ROWS, :]
        gate = nn(a, wg_ref[...])
        up = nn(a, wu_ref[...])
        act = (gate * sigmoid(gate) * up).astype(BF)
        acc[r : r + ROWS, :] += nn(act, wd_ref[...])

    @pl.when(t == tiles - 1)
    def _():
        h = (x_ref[...].astype(F32) + acc[...].astype(BF).astype(F32)).astype(BF)
        h_ref[...] = h
        b = normed(h)
        b_ref[...] = b
        bt_ref[...] = b.T


def forward(x, wg, wu, wd, layer):
    tokens, d = x.shape
    tiles = wg.shape[2] // TILE
    one = lambda s: pl.BlockSpec(s, lambda t: (0, 0))
    return pl.pallas_call(
        functools.partial(forward_kernel, tiles),
        grid=(tiles,),
        in_specs=[
            one((tokens, d)),
            pl.BlockSpec((None, d, TILE), lambda t: (layer, 0, t)),
            pl.BlockSpec((None, d, TILE), lambda t: (layer, 0, t)),
            pl.BlockSpec((None, TILE, d), lambda t: (layer, t, 0)),
        ],
        out_specs=[one((tokens, d)), one((d, tokens)), one((tokens, d)), one((tokens, d)), one((d, tokens))],
        out_shape=[jax.ShapeDtypeStruct(s, BF) for s in ((tokens, d), (d, tokens), (tokens, d), (tokens, d), (d, tokens))],
        scratch_shapes=[pltpu.VMEM((tokens, d), F32)],
        compiler_params=pltpu.CompilerParams(vmem_limit_bytes=60_000_000),
        name="forward",
    )(x, wg, wu, wd)


def places(n):
    me = lax.axis_index("dp")
    chips = n // 2
    z, c = me // 2, lax.rem(me, 2)
    plus = lax.rem(z + 1, chips) * 2 + c
    minus = lax.rem(z + chips - 1, chips) * 2 + c
    return me, z, c, z * 2 + 1 - c, plus, minus


def enter(others):
    barrier = pltpu.get_barrier_semaphore()
    for o in others:
        pl.semaphore_signal(barrier, inc=1, device_id={"dp": o}, device_id_type=MESH)
    pl.semaphore_wait(barrier, len(others))


def backward_kernel(
    n, layers, tiles, rows,
    a0_h, at0_h, a1_h, at1_h, h1_h, dy_h, wg_h, wu_h, wd_h,
    out, squares,
    a, at, h, dy, wg, wu, wd, act, dgate, dup, acc,
    grad, partner_sum, total, hop_in,
    d_send, d_recv, r_send, r_recv, load_sem, w_sem,
):
    chips, half = n // 2, n // 4
    per_layer = tiles * QUARTERS + tiles * 2
    chunks = layers * per_layer
    slots = 2 * LAG
    me, z, c, partner, plus, minus = places(n)
    tokens, d = a.shape

    def load(src, dst, i):
        return pltpu.make_async_copy(src, dst, load_sem.at[i])

    def weights(layer, t, only=None):
        b = lax.rem(t, 2)
        at_cols = pl.ds(pl.multiple_of(t * TILE, TILE), TILE)
        return [
            pltpu.make_async_copy(wg_h.at[layer, :, at_cols], wg.at[b], w_sem.at[0, b]),
            pltpu.make_async_copy(wu_h.at[layer, :, at_cols], wu.at[b], w_sem.at[1, b]),
            pltpu.make_async_copy(wd_h.at[layer, at_cols, :], wd.at[b], w_sem.at[2, b]),
        ]

    first = [load(a1_h, a, 0), load(dy_h, dy, 1), load(at1_h, at, 2), load(h1_h, h, 3)]
    for one in first:
        one.start()
    for one in weights(layers - 1, jnp.int32(0)):
        one.start()
    squares[...] = jnp.zeros_like(squares)
    enter([partner, plus, minus])

    def to_partner(k):
        b = lax.rem(k, RING_PARTNER)
        return pltpu.make_async_remote_copy(
            src_ref=grad.at[lax.rem(k, RING_GRAD), 1 - c],
            dst_ref=partner_sum.at[b],
            send_sem=d_send.at[b],
            recv_sem=d_recv.at[b],
            device_id={"dp": partner},
            device_id_type=MESH,
        )

    def hop(way, s, slot):
        k = lax.rem(slot - LAG_PARTNER - LAG * s, RING_SUM)
        b = lax.rem(slot, slots)
        far = lax.rem(z + (half - s if way == 0 else chips - half + s), chips)
        src, dst = total.at[k, far], hop_in.at[way, s, b]
        if s == 0:
            src, dst = src.at[way], dst.at[way]
        return pltpu.make_async_remote_copy(
            src_ref=src,
            dst_ref=dst,
            send_sem=r_send.at[way, s, b],
            recv_sem=r_recv.at[way, s, b],
            device_id={"dp": plus if way == 0 else minus},
            device_id_type=MESH,
        )

    def during(k):
        return (k >= 0) & (k < chunks)

    def slot(now):
        @pl.when(during(now))
        def _():
            to_partner(now).start()

        k0 = now - LAG_PARTNER

        @pl.when(during(k0))
        def _():
            to_partner(k0).wait()
            i, g, b = lax.rem(k0, RING_SUM), lax.rem(k0, RING_GRAD), lax.rem(k0, RING_PARTNER)
            for j in range(chips):
                total[i, j] = (grad[g, c, j].astype(F32) + partner_sum[b, j].astype(F32)).astype(BF)

        for s in range(1, half):
            k = now - LAG_PARTNER - LAG * s

            @pl.when(during(k))
            def _(k=k, s=s):
                i, b = lax.rem(k, RING_SUM), lax.rem(now - LAG, slots)
                for way in (0, 1):
                    hop(way, s - 1, now - LAG).wait()
                    far = lax.rem(z + (half - s if way == 0 else chips - half + s), chips)
                    if s == 1:
                        total[i, far, way] = (total[i, far, way].astype(F32) + hop_in[way, 0, b, way].astype(F32)).astype(BF)
                    else:
                        total[i, far] = (total[i, far].astype(F32) + hop_in[way, s - 1, b].astype(F32)).astype(BF)

        k1 = now - LAG_PARTNER - LAG * half

        @pl.when(during(k1))
        def _():
            b = lax.rem(now - LAG, slots)
            for way in (0, 1):
                hop(way, half - 1, now - LAG).wait()
            own = total[lax.rem(k1, RING_SUM), z].astype(F32)
            g = (own + hop_in[0, half - 1, b].astype(F32) + hop_in[1, half - 1, b].astype(F32)).astype(BF)
            out[k1] = g
            wide = g.astype(F32)
            squares[...] += wide[0] * wide[0] + wide[1] * wide[1]

        for s in range(half):
            k = now - LAG_PARTNER - LAG * s

            @pl.when(during(k))
            def _(s=s):
                for way in (0, 1):
                    hop(way, s, now).start()

    def elementwise(b, t, r):
        at_rows = pl.ds(r, ROWS)
        gate = nn(a[at_rows, :], wg[b])
        up = nn(a[at_rows, :], wu[b])
        by_act = nt(dy[at_rows, :], wd[b]).astype(BF).astype(F32)
        s = sigmoid(gate)
        silu = gate * s
        act[t, at_rows, :] = (silu * up).astype(BF)
        dup[t, at_rows, :] = (by_act * silu).astype(BF)
        dgate[t, at_rows, :] = (by_act * up * (s * (1.0 + gate * (1.0 - s)))).astype(BF)

    def wide_grad(source, first_chunk, t):
        for p in range(2):
            g = nn(at[p * (d // 2) : (p + 1) * (d // 2), :], source[t])
            for i in range(n // 2):
                dev = p * (n // 2) + i
                for q in range(QUARTERS):
                    k = lax.rem(first_chunk + q // 2, RING_GRAD)
                    grad[k, dev % 2, dev // 2, q % 2] = g[i * rows : (i + 1) * rows, q * LANES : (q + 1) * LANES].astype(BF)

    def tall_grad(t, base):
        acc[:TILE, :] = tn(act[t], dy[...])

        def group(i, _):
            g = t * (TILE // 8) + i
            per_dev = tiles * TILE // n // 8
            dev, rest = g // per_dev, lax.rem(g, per_dev)
            k = lax.rem(base + tiles * QUARTERS + rest // 2, RING_GRAD)
            eight = acc[pl.ds(pl.multiple_of(i * 8, 8), 8), :]
            stacked = jnp.concatenate([eight[:, q * LANES : (q + 1) * LANES] for q in range(d // LANES)], axis=0)
            grad[k, lax.rem(dev, 2), dev // 2, lax.rem(rest, 2)] = stacked.astype(BF)
            return 0

        lax.fori_loop(0, TILE // 8, group, 0, unroll=4)

    def to_states(layer, base):
        for which, (source, w, w_h) in enumerate(((dgate, wg, wg_h), (dup, wu, wu_h))):

            def copy(t, w=w, w_h=w_h, which=which):
                b = lax.rem(t, 2)
                cols = pl.ds(pl.multiple_of(t * TILE, TILE), TILE)
                return pltpu.make_async_copy(w_h.at[layer, :, cols], w.at[b], w_sem.at[which, b])

            copy(jnp.int32(0)).start()
            acc[...] = jnp.zeros_like(acc)

            def one(t, _, source=source, w=w, which=which, copy=copy):
                copy(t).wait()

                @pl.when(t + 1 < tiles)
                def _():
                    copy(t + 1).start()

                for r in range(0, tokens, ROWS):
                    acc[r : r + ROWS, :] += nt(source[t, r : r + ROWS, :], w[lax.rem(t, 2)])

                @pl.when(t < 4)
                def _():
                    slot(base + tiles * QUARTERS + which * 4 + t)

                return 0

            lax.fori_loop(0, tiles, one, 0)
            if which == 0:
                a[...] = acc[...].astype(BF)

        def norm(i, _):
            at_rows = pl.ds(pl.multiple_of(i * 64, 64), 64)
            by_a = (a[at_rows, :].astype(F32) + acc[at_rows, :].astype(BF).astype(F32)).astype(BF).astype(F32)
            wide = h[at_rows, :].astype(F32)
            scale = lax.rsqrt(jnp.mean(wide * wide, -1, keepdims=True) + 1e-6)
            along = jnp.mean(by_a * wide, -1, keepdims=True)
            by_h = (by_a * scale - wide * (scale * scale * scale * along)).astype(BF)
            dy[at_rows, :] = (dy[at_rows, :].astype(F32) + by_h.astype(F32)).astype(BF)
            return 0

        lax.fori_loop(0, tokens // 64, norm, 0)

    for one in first:
        one.wait()
    for step in range(layers):
        layer = layers - 1 - step
        base = step * per_layer

        def tile(t, _, layer=layer, base=base):
            b = lax.rem(t, 2)
            for one in weights(layer, t):
                one.wait()

            @pl.when(t + 1 < tiles)
            def _():
                for one in weights(layer, t + 1):
                    one.start()

            at_chunk = base + t * QUARTERS
            for i, r in enumerate(range(0, tokens, ROWS)):
                elementwise(b, t, r)
                slot(at_chunk - 2 + i)
            wide_grad(dgate, at_chunk, t)
            slot(at_chunk)
            wide_grad(dup, at_chunk + 2, t)
            slot(at_chunk + 1)
            return 0

        lax.fori_loop(0, tiles, tile, 0)
        if step < layers - 1:
            again = [load(at0_h, at, 2)]
            for one in again:
                one.start()

        def down(t, _, base=base):
            tall_grad(t, base)

            @pl.when(lax.rem(t, 2) == 1)
            def _():
                slot(base + tiles * QUARTERS - 2 + t // 2)

            return 0

        lax.fori_loop(0, tiles, down, 0)
        if step < layers - 1:
            to_states(layer, base)
            more = load(a0_h, a, 0)
            more.start()
            for one in weights(layer - 1, jnp.int32(0)):
                one.start()
            more.wait()
            for one in again:
                one.wait()

    def rest(i, _):
        slot(i)
        return 0

    lax.fori_loop((layers - 1) * per_layer + tiles * QUARTERS, chunks + LAG_PARTNER + LAG * half, rest, 0)


def backward(n, a0, at0, a1, at1, h1, dy, wg, wu, wd):
    layers, d, ff = wg.shape
    tokens = dy.shape[0]
    tiles, rows, chips, half = ff // TILE, d // n, n // 2, n // 4
    chunks = layers * (tiles * QUARTERS + tiles * 2)
    unit = (2, rows, LANES)
    hbm, vmem = pl.BlockSpec(memory_space=pl.ANY), pl.BlockSpec(memory_space=pltpu.VMEM)
    return pl.pallas_call(
        functools.partial(backward_kernel, n, layers, tiles, rows),
        in_specs=[hbm] * 9,
        out_specs=[vmem] * 2,
        out_shape=[jax.ShapeDtypeStruct((chunks,) + unit, BF), jax.ShapeDtypeStruct((rows, LANES), F32)],
        scratch_shapes=[
            pltpu.VMEM((tokens, d), BF),
            pltpu.VMEM((d, tokens), BF),
            pltpu.VMEM((tokens, d), BF),
            pltpu.VMEM((tokens, d), BF),
            pltpu.VMEM((2, d, TILE), BF),
            pltpu.VMEM((2, d, TILE), BF),
            pltpu.VMEM((2, TILE, d), BF),
            pltpu.VMEM((tiles, tokens, TILE), BF),
            pltpu.VMEM((tiles, tokens, TILE), BF),
            pltpu.VMEM((tiles, tokens, TILE), BF),
            pltpu.VMEM((tokens, d), F32),
            pltpu.VMEM((RING_GRAD, 2, chips) + unit, BF),
            pltpu.VMEM((RING_PARTNER, chips) + unit, BF),
            pltpu.VMEM((RING_SUM, chips) + unit, BF),
            pltpu.VMEM((2, half, 2 * LAG) + unit, BF),
            pltpu.SemaphoreType.DMA((RING_PARTNER,)),
            pltpu.SemaphoreType.DMA((RING_PARTNER,)),
            pltpu.SemaphoreType.DMA((2, half, 2 * LAG)),
            pltpu.SemaphoreType.DMA((2, half, 2 * LAG)),
            pltpu.SemaphoreType.DMA((4,)),
            pltpu.SemaphoreType.DMA((3, 2)),
        ],
        compiler_params=pltpu.CompilerParams(collective_id=0, has_side_effects=True, vmem_limit_bytes=VMEM_LIMIT),
        name="backward",
    )(a0, at0, a1, at1, h1, dy, wg, wu, wd)


def update_kernel(n, layers, tiles, count, *refs):
    grads, squares = refs[:2]
    w_h, m_h, v_h = refs[2:5], refs[5:8], refs[8:11]
    w_out, m_out, v_out = refs[11:14], refs[14:17], refs[17:20]
    w_in, m_in, v_in = refs[20:23], refs[23:26], refs[26:29]
    everyone, load_sem, store_sem, s_send, s_recv, r_send, r_recv, d_send, d_recv = refs[29:]
    chips, half = n // 2, n // 4
    me, z, c, partner, plus, minus = places(n)
    per_layer = grads.shape[0] // layers
    pieces = [(layer, i) for layer in range(layers) for i in range(3)]

    def own(ref, layer, i):
        rows = m_in[i].shape[1]
        return ref.at[layer, pl.ds(pl.multiple_of(me * rows, 8), rows), :]

    loads = []
    for p, (layer, i) in enumerate(pieces):
        loads.append(
            [
                pltpu.make_async_copy(own(w_h[i], layer, i), w_in[i].at[layer], load_sem.at[p, 0]),
                pltpu.make_async_copy(m_h[i].at[layer], m_in[i].at[layer], load_sem.at[p, 1]),
                pltpu.make_async_copy(v_h[i].at[layer], v_in[i].at[layer], load_sem.at[p, 2]),
            ]
        )
        for one in loads[-1]:
            one.start()
    everyone[me] = jnp.sum(squares[...].reshape(-1, 8, LANES), axis=0)
    enter([lax.rem(me + i, n) for i in range(1, n)])
    shares = []
    for i in range(1, n):
        shares.append(
            pltpu.make_async_remote_copy(
                src_ref=everyone.at[me],
                dst_ref=everyone.at[me],
                send_sem=s_send.at[i - 1],
                recv_sem=s_recv.at[i - 1],
                device_id={"dp": lax.rem(me + i, n)},
                device_id_type=MESH,
            )
        )
        shares[-1].start()
    for i in range(1, n):
        source = lax.rem(me + n - i, n)
        pltpu.make_async_remote_copy(
            src_ref=everyone.at[source],
            dst_ref=everyone.at[source],
            send_sem=s_send.at[i - 1],
            recv_sem=s_recv.at[i - 1],
            device_id={"dp": lax.rem(me + i, n)},
            device_id_type=MESH,
        ).wait_recv()
    square = jnp.sum(everyone[...])
    factor = jnp.minimum(1.0, 0.5 * lax.rsqrt(square / count + 1e-30))

    def step(w, m, v, g):
        g = g.astype(F32) * factor
        m = 0.9 * m + 0.1 * g
        v = 0.95 * v + 0.05 * g * g
        w = w.astype(F32)
        return (w - 0.02 * (m * lax.rsqrt(v + 1e-8) + 0.1 * w)).astype(BF), m, v

    def block(ref, p, chip, core, part=None):
        layer, i = pieces[p]
        rows, cols = m_in[i].shape[1:]
        start = (chip * 2 + core) * rows
        if part is None:
            return ref.at[layer, pl.ds(pl.multiple_of(start, 8), rows), :]
        if i == 2:
            return ref.at[layer, pl.ds(pl.multiple_of(start + part * (rows // 2), 8), rows // 2), :]
        return ref.at[layer, pl.ds(pl.multiple_of(start, 8), rows), pl.ds(part * (cols // 2), cols // 2)]

    def part_of(ref, p, part):
        layer, i = pieces[p]
        rows, cols = m_in[i].shape[1:]
        if i == 2:
            return ref.at[layer, pl.ds(part * (rows // 2), rows // 2), :]
        return ref.at[layer, :, pl.ds(part * (cols // 2), cols // 2)]

    def hop(way, s, p):
        i = pieces[p][1]
        chip = lax.rem(z + (chips - s if way == 0 else s), chips)
        part = way if s == half - 1 else None
        dst = block(w_out[i], p, chip, c, part)
        if s == 0:
            src = w_in[i].at[pieces[p][0]] if part is None else part_of(w_in[i], p, part)
        else:
            src = dst
        return pltpu.make_async_remote_copy(
            src_ref=src,
            dst_ref=dst,
            send_sem=r_send.at[way, s, p],
            recv_sem=r_recv.at[way, s, p],
            device_id={"dp": plus if way == 0 else minus},
            device_id_type=MESH,
        )

    def across(j, p):
        i = pieces[p][1]
        if j == 0:
            src, dst = w_in[i].at[pieces[p][0]], block(w_out[i], p, z, c)
        else:
            s, way = (j - 1) // 2, (j - 1) % 2
            chip = lax.rem(z + (chips - 1 - s if way == 0 else 1 + s), chips)
            dst = block(w_out[i], p, chip, c, way if s == half - 1 else None)
            src = dst
        return pltpu.make_async_remote_copy(
            src_ref=src,
            dst_ref=dst,
            send_sem=d_send.at[j, p],
            recv_sem=d_recv.at[j, p],
            device_id={"dp": partner},
            device_id_type=MESH,
        )

    stores = []
    for p, (layer, i) in enumerate(pieces):
        for one in loads[p]:
            one.wait()
        base = (layers - 1 - layer) * per_layer
        rows, cols = m_in[i].shape[1:]
        w1, m1, v1 = w_in[i], m_in[i], v_in[i]
        if i < 2:

            def column(q, _, base=base, layer=layer, i=i, w1=w1, m1=m1, v1=v1):
                t, r = q // QUARTERS, lax.rem(q, QUARTERS)
                at_cols = pl.ds(pl.multiple_of(q * LANES, LANES), LANES)
                g = grads[base + t * QUARTERS + 2 * i + r // 2, lax.rem(r, 2)]
                w, m, v = step(w1[layer, :, at_cols], m1[layer, :, at_cols], v1[layer, :, at_cols], g)
                w1[layer, :, at_cols] = w
                m1[layer, :, at_cols] = m
                v1[layer, :, at_cols] = v
                return 0

            lax.fori_loop(0, cols // LANES, column, 0)
        else:

            def row(j, _, base=base, layer=layer, w1=w1, m1=m1, v1=v1):
                at_rows = pl.ds(pl.multiple_of(j * 16, 16), 16)
                g = grads[base + tiles * QUARTERS + j].astype(F32)
                g = jnp.concatenate(
                    [jnp.concatenate([g[r, 8 * q : 8 * q + 8, :] for q in range(cols // LANES)], axis=1) for r in (0, 1)], axis=0
                )
                w, m, v = step(w1[layer, at_rows, :], m1[layer, at_rows, :], v1[layer, at_rows, :], g)
                w1[layer, at_rows, :] = w
                m1[layer, at_rows, :] = m
                v1[layer, at_rows, :] = v
                return 0

            lax.fori_loop(0, rows // 16, row, 0)
        stores.append(pltpu.make_async_copy(m1.at[layer], m_out[i].at[layer], store_sem.at[p, 0]))
        stores.append(pltpu.make_async_copy(v1.at[layer], v_out[i].at[layer], store_sem.at[p, 1]))
        stores.append(pltpu.make_async_copy(w1.at[layer], block(w_out[i], p, z, c), store_sem.at[p, 2]))
        for way in (0, 1):
            hop(way, 0, p).start()
        across(0, p).start()
        for one in stores[-3:]:
            one.start()
    for s in range(1, half + 1):
        for p in range(len(pieces)):
            for way in (0, 1):
                hop(way, s - 1, p).wait_recv()
                if s < half:
                    hop(way, s, p).start()
                across(1 + 2 * (s - 1) + way, p).start()
    for one in stores:
        one.wait()
    for p in range(len(pieces)):
        for j in range(1 + 2 * half):
            across(j, p).wait()
        for s in range(half):
            for way in (0, 1):
                hop(way, s, p).wait_send()
    for one in shares:
        one.wait_send()


def update(n, grads, squares, ws, ms, vs):
    layers, d, ff = ws[0].shape
    half = n // 4
    pieces = 3 * layers
    tiles = ff // TILE
    hbm, vmem = pl.BlockSpec(memory_space=pl.ANY), pl.BlockSpec(memory_space=pltpu.VMEM)
    count = sum(w.size for w in ws)
    like = lambda t, dt=None: jax.ShapeDtypeStruct(t.shape, dt or t.dtype)
    return pl.pallas_call(
        functools.partial(update_kernel, n, layers, tiles, count),
        in_specs=[vmem, vmem] + [hbm] * 9,
        out_specs=[hbm] * 9,
        out_shape=[like(t) for t in (*ws, *ms, *vs)],
        scratch_shapes=[pltpu.VMEM(m.shape, BF) for m in ms]
        + [pltpu.VMEM(m.shape, F32) for m in ms]
        + [pltpu.VMEM(v.shape, F32) for v in vs]
        + [
            pltpu.VMEM((n, 8, LANES), F32),
            pltpu.SemaphoreType.DMA((pieces, 3)),
            pltpu.SemaphoreType.DMA((pieces, 3)),
            pltpu.SemaphoreType.DMA((n - 1,)),
            pltpu.SemaphoreType.DMA((n - 1,)),
            pltpu.SemaphoreType.DMA((2, half, pieces)),
            pltpu.SemaphoreType.DMA((2, half, pieces)),
            pltpu.SemaphoreType.DMA((1 + 2 * half, pieces)),
            pltpu.SemaphoreType.DMA((1 + 2 * half, pieces)),
        ],
        compiler_params=pltpu.CompilerParams(collective_id=1, has_side_effects=True, vmem_limit_bytes=40_000_000),
        name="update",
    )(grads, squares, *ws, *ms, *vs)


def solution(mesh):
    n = mesh.shape["dp"]

    def of_a_device(x, dy, *arrays):
        ws, ms, vs = (arrays[i : i + 3] for i in (0, 3, 6))
        a0, at0, h1, a1, at1 = forward(x[0], *ws, 0)
        grads, squares = backward(n, a0, at0, a1, at1, h1, dy[0], *ws)
        return tuple(update(n, grads, squares, ws, ms, vs))

    seq, whole, rows = P(("rep", "dp")), P(), P(None, "dp")
    return jax.shard_map(
        of_a_device,
        mesh=mesh,
        in_specs=(seq, seq) + (whole,) * 3 + (rows,) * 6,
        out_specs=(P("rep"),) * 3 + (P("rep", "dp"),) * 6,
        check_vma=False,
    )
```

time: 747 us -> 420 us (0.56)
  waiting for transfers between devices: 462 us -> 0 us
  Pallas kernels: 0 us -> 374 us
  matrix products: 168 us -> 0 us
  other arithmetic: 27.5 us -> 0 us
  blocking collectives: 27.5 us -> 0 us
  between operations: 19 us -> 0.69 us
  local copies, waits for them, and re-layouts: 35.8 us -> 44.6 us
    pallas_call x0 -> x3, Pallas kernels: none -> 374 us  [the longest x1 196 us: backward(): pl.pallas_call(functools.partial(backward_kernel, n, layers, tiles, rows)...]
    reduce_scatter x6 -> x0, waiting for transfers between devices: 300 us -> none  [of_a_device(): lax.psum_scatter(terms[i][n], 'dp', scatter_dimension=0, tiled=True)]
    dot_general x15 -> x0, matrix products: 168 us -> none  [the longest x5 60 us: layer(): gate = jnp.dot(a, w['w_gate'], preferred_element_type=jnp.float32)]
    all_gather x3 -> x0, waiting for transfers between devices: 161 us -> none  [of_a_device(): new.append((lax.all_gather(w1, 'dp', axis=1, tiled=True), m1, v1))]
    psum x1 -> x0, blocking collectives: 27.5 us -> none  [of_a_device(): lax.psum(sum((jnp.sum(g * g) for one in sums for g in one.values())), 'dp')]
    reduce_sum x7 -> x0, other arithmetic: 10.7 us -> none  [the longest x6 10.3 us: of_a_device(): jnp.sum(g * g)]
    convert_element_type x3 -> x0, other arithmetic: 9.48 us -> none  [adamw(): return ((w - 0.02 * step).astype(jnp.bfloat16), m, v)]
    unnamed x47 -> x35, local copies, waits for them, and re-layouts: 35.8 us -> 44.6 us
  transfers between devices with their start and end apart: 9 -> 0, of which waited for: 9 -> 0; matrix products, arithmetic and copies ran while one was open for 10% -> 0% of each run, Pallas kernels for 0% -> 0%
where the time goes in v2:
time: 420 us; the launch traced here: 419 us
  Pallas kernels  374 us (89%)
  local copies, waits for them, and re-layouts  44.6 us (11%)
    pallas_call x1, Pallas kernels, backward(): pl.pallas_call(functools.partial(backward_kernel, n, layers, tiles, rows)...  196 us
    pallas_call x1, Pallas kernels, update(): pl.pallas_call(functools.partial(update_kernel, n, layers, tiles, count),...  151 us
    unnamed x35, local copies, waits for them, and re-layouts  44.6 us
    pallas_call x1, Pallas kernels, forward(): pl.pallas_call(functools.partial(forward_kernel, tiles), grid=(tiles,), i...  27.1 us

profile of v2, /device:TPU:21, one launch (start us, length us, event | category | flops | bytes accessed | tf_op | source)
XLA Modules:
  0.0 419.2 jit_solution(11623544095626520661)
XLA Ops:
  0.6 27.1 %forward.1 = (bf16[1024,896]{1,0:T(8,128)(2,1)}, bf16[896,1024]{1,0:T(8,128)(2,1)}, bf16[1024,896]{1,0:T(8,128)(2,1)}, bf16[1024,896]{1,0:T(8,128)(2,1)}, bf16[896,1024]{1,0:T(8,128)(2,1)}) custom-call(bf16[1024,896]{1,0:T(8,128)(2,1)} %bitcast.2, bf16[2,896,2560]{2,1,0:T(8,128)(2,1)} %refs_2_.1, bf16[2,896,2560]{2,1,0:T(8,128)(2,1)} %refs_3_.1, ...), custom_call_target="tpu_custom_call" | custom-call | tf_op jit(solution)/shard_map/forward/pallas_call | solution.py:74
  27.7 196.1 %backward.1 = (bf16[60,2,56,128]{3,2,1,0:T(8,128)(2,1)}, f32[56,128]{1,0:T(8,128)}) custom-call(bf16[1024,896]{1,0:T(8,128)(2,1)} %get-tuple-element.16.a0_h, bf16[896,1024]{1,0:T(8,128)(2,1)} %get-tuple-element.17.at0_h, bf16[1024,896]{1,0:T(8,128)(2,1)} %get-tuple-element.18.a1_h, bf16[896,1024]{1,0:T(8,128)(2,1)} %get-tuple-element.19.at1_h, ...), custom_call_target="tpu_custom_call" | custom-call | tf_op jit(solution)/shard_map/backward/pallas_call | solution.py:365
  223.8 0.0 copy-start
  223.8 1.5 copy-done
  225.3 0.0 copy-start.6
  225.3 1.3 copy-done.6
  226.5 0.0 copy-start.7
  226.5 1.3 copy-done.7
  227.8 0.0 copy-start.8
  227.8 1.3 copy-done.8
  229.0 0.0 copy-start.9
  229.1 1.3 copy-done.9
  230.3 0.0 copy-start.10
  230.3 1.3 copy-done.10
  231.6 0.0 copy-start.11
  231.6 1.3 copy-done.11
  232.8 0.0 copy-start.12
  232.8 0.7 copy-done.12
  233.6 150.8 %update.1 = (bf16[2,896,2560]{2,1,0:T(8,128)(2,1)}, bf16[2,896,2560]{2,1,0:T(8,128)(2,1)}, bf16[2,2560,896]{2,1,0:T(8,128)(2,1)}, f32[2,56,2560]{2,1,0:T(8,128)S...) custom-call(bf16[60,2,56,128]{3,2,1,0:T(8,128)(2,1)S(1)} %copy-done,, ...), custom_call_target="tpu_custom_call" | custom-call | tf_op jit(solution)/shard_map/update/pallas_call | solution.py:582
  384.3 0.0 copy-start.1
  384.4 1.0 copy-done.1
  385.4 0.0 copy-start.3
  385.4 1.0 copy-done.3
  386.4 0.0 copy-start.5
  386.4 1.0 copy-done.5
  387.4 7.8 %copy.29 = bf16[2,896,2560]{2,1,0:T(8,128)(2,1)} copy(bf16[2,896,2560]{2,1,0:T(8,128)(2,1)} %get-tuple-element.32) | data formatting | bytes 18350080
  395.2 7.8 %copy.30 = bf16[2,896,2560]{2,1,0:T(8,128)(2,1)} copy(bf16[2,896,2560]{2,1,0:T(8,128)(2,1)} %get-tuple-element.33) | data formatting | bytes 18350080
  403.1 8.0 %copy.31 = bf16[2,2560,896]{2,1,0:T(8,128)(2,1)} copy(bf16[2,2560,896]{2,1,0:T(8,128)(2,1)} %get-tuple-element.34) | data formatting | bytes 18350080
  411.0 0.0 copy-start.4
  411.1 2.4 copy.32
  413.5 0.0 copy-done.4
  413.5 0.0 copy-start.2
  413.5 1.0 copy.33
  414.5 0.7 copy-done.2
  415.2 1.0 copy.34
  416.2 1.0 copy.35
  417.2 1.0 copy.36
  418.2 1.0 copy.37
Async XLA Ops:
  223.8 1.5 copy-start
  225.3 1.3 copy-start.6
  226.5 1.3 copy-start.7
  227.8 1.3 copy-start.8
  229.0 1.3 copy-start.9
  230.3 1.3 copy-start.10
  231.6 1.3 copy-start.11
  232.8 0.7 copy-start.12
  384.3 1.0 copy-start.1
  385.4 1.0 copy-start.3
  386.4 1.0 copy-start.5
  411.0 2.4 copy-start.4
  413.5 1.7 copy-start.2

commit v3 on v2

v3 whole, which is shorter than its diff:
```python
import functools

import jax
import jax.numpy as jnp
from jax import lax
from jax.experimental import pallas as pl
from jax.experimental.pallas import tpu as pltpu
from jax.sharding import PartitionSpec as P

MESH = pl.DeviceIdType.MESH
BF, F32 = jnp.bfloat16, jnp.float32
LANES = 128
TILE = 512
QUARTERS = TILE // LANES
ROWS = 256
LAG = 2
LAG_PARTNER = 1
RING_GRAD, RING_SUM, RING_PARTNER = 4, 10, 4
VMEM_LIMIT = 62_000_000


def nn(a, b):
    return lax.dot_general(a, b, (((1,), (0,)), ((), ())), preferred_element_type=F32)


def nt(a, b):
    return lax.dot_general(a, b, (((1,), (1,)), ((), ())), preferred_element_type=F32)


def tn(a, b):
    return lax.dot_general(a, b, (((0,), (0,)), ((), ())), preferred_element_type=F32)


def normed(h):
    wide = h.astype(F32)
    scale = lax.rsqrt(jnp.mean(wide * wide, -1, keepdims=True) + 1e-6)
    return (wide * scale).astype(BF)


def sigmoid(x):
    return 1.0 / (1.0 + jnp.exp(-x))


def places(n):
    me = lax.axis_index("dp")
    chips = n // 2
    z, c = me // 2, lax.rem(me, 2)
    plus = lax.rem(z + 1, chips) * 2 + c
    minus = lax.rem(z + chips - 1, chips) * 2 + c
    return me, z, c, z * 2 + 1 - c, plus, minus


def greet(others):
    for o in others:
        pl.semaphore_signal(pltpu.get_barrier_semaphore(), inc=1, device_id={"dp": o}, device_id_type=MESH)


def meet(count):
    pl.semaphore_wait(pltpu.get_barrier_semaphore(), count)


def backward_kernel(
    n, layers, tiles, rows,
    x_h, dy_h, wg_h, wu_h, wd_h,
    out, square,
    h, a0, a1, at, dy, wg, wu, wd, act, dgate, dup, acc,
    grad, partner_sum, total, hop_in, squares, everyone,
    d_send, d_recv, r_send, r_recv, s_send, s_recv, load_sem, wide_sem, tall_sem,
):
    chips, half = n // 2, n // 4
    per_layer = 3 * tiles
    chunks = layers * per_layer
    slots = 2 * LAG
    full = LAG_PARTNER + LAG * half
    me, z, c, partner, plus, minus = places(n)
    tokens, d = h.shape

    def wide_weight(i, layer, t):
        w_h, w = ((wg_h, wg), (wu_h, wu))[i]
        at_tile = pl.ds(pl.multiple_of(t * TILE, TILE), TILE)
        return pltpu.make_async_copy(w_h.at[layer, :, at_tile], w.at[t], wide_sem.at[i, t])

    def wide_weights(layer, t):
        return [wide_weight(i, layer, t) for i in (0, 1)]

    def tall_weights(layer, t, turn):
        b = lax.rem(turn, 2)
        at_tile = pl.ds(pl.multiple_of(t * TILE, TILE), TILE)
        return pltpu.make_async_copy(wd_h.at[layer, at_tile, :], wd.at[b], tall_sem.at[b])

    def each_tile(what):
        def body(t, _):
            what(t)
            return 0

        lax.fori_loop(0, tiles, body, 0)

    def start(copies):
        for one in copies:
            one.start()

    def wait(copies):
        for one in copies:
            one.wait()

    def next_tall(layer, t, turn, after):
        tall_weights(layer, t, turn).wait()

        @pl.when(t + 1 < tiles)
        def _():
            tall_weights(layer, t + 1, turn + 1).start()

        if after is not None:

            @pl.when(t + 1 == tiles)
            def _():
                tall_weights(after, jnp.int32(0), turn + 1).start()

    load_x = pltpu.make_async_copy(x_h, h, load_sem.at[0])
    load_dy = pltpu.make_async_copy(dy_h, dy, load_sem.at[1])
    load_x.start()
    start(wide_weights(0, jnp.int32(0)))
    tall_weights(0, jnp.int32(0), jnp.int32(0)).start()
    for t in range(1, tiles):
        start(wide_weights(0, jnp.int32(t)))
    load_dy.start()
    others = [lax.rem(me + i, n) for i in range(1, n)]
    greet(others)
    squares[...] = jnp.zeros_like(squares)
    acc[...] = jnp.zeros_like(acc)

    def place_of(k):
        within = lax.rem(k, per_layer)
        tall = within // (2 * tiles)
        return tall * (within - 2 * tiles + RING_GRAD) + (1 - tall) * lax.rem(within, RING_GRAD)

    def to_partner(k):
        b = lax.rem(k, RING_PARTNER)
        return pltpu.make_async_remote_copy(
            src_ref=grad.at[place_of(k), 1 - c],
            dst_ref=partner_sum.at[b],
            send_sem=d_send.at[b],
            recv_sem=d_recv.at[b],
            device_id={"dp": partner},
            device_id_type=MESH,
        )

    def target(way, s):
        return lax.rem(z + (half - s if way == 0 else chips - half + s), chips)

    def hop(way, s, slot):
        k = lax.rem(slot - LAG_PARTNER - LAG * s, RING_SUM)
        b = lax.rem(slot, slots)
        src, dst = total.at[k, target(way, s)], hop_in.at[way, s, b]
        if s == 0:
            src, dst = src.at[way], dst.at[way]
        return pltpu.make_async_remote_copy(
            src_ref=src,
            dst_ref=dst,
            send_sem=r_send.at[way, s, b],
            recv_sem=r_recv.at[way, s, b],
            device_id={"dp": plus if way == 0 else minus},
            device_id_type=MESH,
        )

    def add_partner(k):
        i, g, b = lax.rem(k, RING_SUM), place_of(k), lax.rem(k, RING_PARTNER)
        for j in range(chips):
            total[i, j] = (grad[g, c, j].astype(F32) + partner_sum[b, j].astype(F32)).astype(BF)

    def add_hop(way, s, k, now):
        i, b, far = lax.rem(k, RING_SUM), lax.rem(now - LAG, slots), target(way, s)
        if s == 1:
            total[i, far, way] = (total[i, far, way].astype(F32) + hop_in[way, 0, b, way].astype(F32)).astype(BF)
        else:
            total[i, far] = (total[i, far].astype(F32) + hop_in[way, s - 1, b].astype(F32)).astype(BF)

    def finish(k, now):
        b = lax.rem(now - LAG, slots)
        own = total[lax.rem(k, RING_SUM), z].astype(F32)
        g = (own + hop_in[0, half - 1, b].astype(F32) + hop_in[1, half - 1, b].astype(F32)).astype(BF)
        out[k] = g
        wide = g.astype(F32)
        squares[...] += wide[0, 0] * wide[0, 0] + wide[0, 1] * wide[0, 1] + wide[1, 0] * wide[1, 0] + wide[1, 1] * wide[1, 1]

    def slot(now):
        ks = [now - LAG_PARTNER - LAG * s for s in range(half + 1)]
        filled = (ks[half] >= 0) & (now < chunks)

        @pl.when(filled)
        def _():
            to_partner(now).start()
            to_partner(ks[0]).wait()
            for s in range(1, half + 1):
                for way in (0, 1):
                    hop(way, s - 1, now - LAG).wait()
            add_partner(ks[0])
            for s in range(1, half):
                for way in (0, 1):
                    add_hop(way, s, ks[s], now)
            finish(ks[half], now)
            for s in range(half):
                for way in (0, 1):
                    hop(way, s, now).start()

        @pl.when(jnp.logical_not(filled))
        def _():
            def during(k):
                return (k >= 0) & (k < chunks)

            @pl.when(during(now))
            def _():
                to_partner(now).start()

            @pl.when(during(ks[0]))
            def _():
                to_partner(ks[0]).wait()
                add_partner(ks[0])

            for s in range(1, half + 1):

                @pl.when(during(ks[s]))
                def _(s=s):
                    for way in (0, 1):
                        hop(way, s - 1, now - LAG).wait()
                    if s < half:
                        for way in (0, 1):
                            add_hop(way, s, ks[s], now)
                    else:
                        finish(ks[s], now)

            for s in range(half):

                @pl.when(during(ks[s]))
                def _(s=s):
                    for way in (0, 1):
                        hop(way, s, now).start()

    def forward(b, a, t):
        for r in range(0, tokens, ROWS):
            mine = a[r : r + ROWS, :]
            gate = nn(mine, wg[t])
            up = nn(mine, wu[t])
            hidden = (gate * sigmoid(gate) * up).astype(BF)
            acc[r : r + ROWS, :] += nn(hidden, wd[b])

    def elementwise(b, a, t):
        for r in range(0, tokens, ROWS):
            at_rows = pl.ds(r, ROWS)
            gate = nn(a[at_rows, :], wg[t])
            up = nn(a[at_rows, :], wu[t])
            by_act = nt(dy[at_rows, :], wd[b]).astype(BF).astype(F32)
            s = sigmoid(gate)
            silu = gate * s
            act[t, at_rows, :] = (silu * up).astype(BF)
            dup[t, at_rows, :] = (by_act * silu).astype(BF)
            dgate[t, at_rows, :] = (by_act * up * (s * (1.0 + gate * (1.0 - s)))).astype(BF)

    def wide_grad(source, chunk, t):
        k = place_of(chunk)
        for p in range(2):
            g = nn(at[p * (d // 2) : (p + 1) * (d // 2), :], source[t])
            for i in range(n // 2):
                dev = p * (n // 2) + i
                for q in range(QUARTERS):
                    grad[k, dev % 2, dev // 2, q // 2, q % 2] = g[i * rows : (i + 1) * rows, q * LANES : (q + 1) * LANES].astype(BF)

    def tall_grad(t):
        acc[:TILE, :] = tn(act[t], dy[...])
        per_dev = tiles * TILE // n // 8

        def group(i, _):
            g = t * (TILE // 8) + i
            dev, rest = g // per_dev, lax.rem(g, per_dev)
            k = RING_GRAD + rest // 4
            eight = acc[pl.ds(pl.multiple_of(i * 8, 8), 8), :]
            stacked = jnp.concatenate([eight[:, q * LANES : (q + 1) * LANES] for q in range(d // LANES)], axis=0)
            quarter = lax.rem(rest, 4)
            grad[k, lax.rem(dev, 2), dev // 2, quarter // 2, lax.rem(quarter, 2)] = stacked.astype(BF)
            return 0

        lax.fori_loop(0, TILE // 8, group, 0, unroll=8)

    def to_states(layer, a, first_slot):
        turn = 0
        for source, w, w_h in ((dgate, wg, wg_h), (dup, wu, wu_h)):
            for r in range(0, tokens, tokens // 2):
                at_rows = pl.ds(r, tokens // 2)
                part = nt(source[0, at_rows, :], w[0])
                for t in range(1, tiles):
                    part += nt(source[t, at_rows, :], w[t])
                if source is dgate:
                    a[at_rows, :] = part.astype(BF)
                else:
                    acc[at_rows, :] = part
                slot(first_slot + turn)
                turn += 1
            which = 0 if source is dgate else 1
            for t in range(tiles):
                wide_weight(which, layer - 1, jnp.int32(t)).start()

        def norm(i, _):
            at_rows = pl.ds(pl.multiple_of(i * 64, 64), 64)
            by_a = (a[at_rows, :].astype(F32) + acc[at_rows, :].astype(BF).astype(F32)).astype(BF).astype(F32)
            wide = h[at_rows, :].astype(F32)
            scale = lax.rsqrt(jnp.mean(wide * wide, -1, keepdims=True) + 1e-6)
            along = jnp.mean(by_a * wide, -1, keepdims=True)
            by_h = (by_a * scale - wide * (scale * scale * scale * along)).astype(BF)
            dy[at_rows, :] = (dy[at_rows, :].astype(F32) + by_h.astype(F32)).astype(BF)
            return 0

        lax.fori_loop(0, tokens // 64, norm, 0)
        slot(first_slot + turn)

    load_x.wait()
    for r in range(0, tokens, 128):
        a0[r : r + 128, :] = normed(h[r : r + 128, :])

    def ahead(t):
        wait(wide_weights(0, t))
        next_tall(0, t, t, layers - 1)
        forward(lax.rem(t, 2), a0, t)
        start(wide_weights(layers - 1, t))

    each_tile(ahead)
    for r in range(0, tokens, 128):
        new = (h[r : r + 128, :].astype(F32) + acc[r : r + 128, :].astype(BF).astype(F32)).astype(BF)
        h[r : r + 128, :] = new
        a1[r : r + 128, :] = normed(new)
    at[...] = a1[...].T
    load_dy.wait()
    meet(n - 1)

    for step in range(layers):
        layer = layers - 1 - step
        base = step * per_layer
        a = (a0, a1)[layer]

        def tile(t, layer=layer, base=base, a=a, step=step):
            turn = (step + 1) * tiles + t
            wait(wide_weights(layer, t))
            next_tall(layer, t, turn, layer - 1 if layer > 0 else None)
            chunk = base + 2 * t
            elementwise(lax.rem(turn, 2), a, t)
            slot(chunk - 1)
            wide_grad(dgate, chunk, t)
            slot(chunk)
            wide_grad(dup, chunk + 1, t)
            tall_grad(t)

        each_tile(tile)
        if step < layers - 1:
            to_states(layer, a, base + 2 * tiles - 1)
            at[...] = a0[...].T

    def rest(i, _):
        slot(i)
        return 0

    lax.fori_loop((layers - 1) * per_layer + 2 * tiles - 1, chunks + full, rest, 0)

    everyone[me] = jnp.sum(squares[...].reshape(-1, 8, LANES), axis=0)

    def share(i, source):
        return pltpu.make_async_remote_copy(
            src_ref=everyone.at[source],
            dst_ref=everyone.at[source],
            send_sem=s_send.at[i],
            recv_sem=s_recv.at[i],
            device_id={"dp": others[i]},
            device_id_type=MESH,
        )

    for i in range(n - 1):
        share(i, me).start()
    for i in range(n - 1):
        share(i, lax.rem(me + n - 1 - i, n)).wait_recv()
    square[...] = jnp.sum(everyone[...], axis=0)
    for i in range(n - 1):
        share(i, me).wait_send()


def backward(n, x, dy, wg, wu, wd):
    layers, d, ff = wg.shape
    tokens = dy.shape[0]
    tiles, rows, chips, half = ff // TILE, d // n, n // 2, n // 4
    chunks = 3 * layers * tiles
    unit = (2, 2, rows, LANES)
    hbm, vmem = pl.BlockSpec(memory_space=pl.ANY), pl.BlockSpec(memory_space=pltpu.VMEM)
    return pl.pallas_call(
        functools.partial(backward_kernel, n, layers, tiles, rows),
        in_specs=[hbm] * 5,
        out_specs=[vmem] * 2,
        out_shape=[pltpu.VMEM((chunks,) + unit, BF), pltpu.VMEM((8, LANES), F32)],
        scratch_shapes=[
            pltpu.VMEM((tokens, d), BF),
            pltpu.VMEM((tokens, d), BF),
            pltpu.VMEM((tokens, d), BF),
            pltpu.VMEM((d, tokens), BF),
            pltpu.VMEM((tokens, d), BF),
            pltpu.VMEM((tiles, d, TILE), BF),
            pltpu.VMEM((tiles, d, TILE), BF),
            pltpu.VMEM((2, TILE, d), BF),
            pltpu.VMEM((tiles, tokens, TILE), BF),
            pltpu.VMEM((tiles, tokens, TILE), BF),
            pltpu.VMEM((tiles, tokens, TILE), BF),
            pltpu.VMEM((tokens, d), F32),
            pltpu.VMEM((RING_GRAD + tiles, 2, chips) + unit, BF),
            pltpu.VMEM((RING_PARTNER, chips) + unit, BF),
            pltpu.VMEM((RING_SUM, chips) + unit, BF),
            pltpu.VMEM((2, half, 2 * LAG) + unit, BF),
            pltpu.VMEM((rows, LANES), F32),
            pltpu.VMEM((n, 8, LANES), F32),
            pltpu.SemaphoreType.DMA((RING_PARTNER,)),
            pltpu.SemaphoreType.DMA((RING_PARTNER,)),
            pltpu.SemaphoreType.DMA((2, half, 2 * LAG)),
            pltpu.SemaphoreType.DMA((2, half, 2 * LAG)),
            pltpu.SemaphoreType.DMA((n - 1,)),
            pltpu.SemaphoreType.DMA((n - 1,)),
            pltpu.SemaphoreType.DMA((2,)),
            pltpu.SemaphoreType.DMA((2, tiles)),
            pltpu.SemaphoreType.DMA((2,)),
        ],
        compiler_params=pltpu.CompilerParams(collective_id=0, has_side_effects=True, vmem_limit_bytes=VMEM_LIMIT),
        name="backward",
    )(x, dy, wg, wu, wd)


def update_kernel(n, layers, tiles, count, *refs):
    grads, square = refs[:2]
    w_h, m_h, v_h = refs[2:5], refs[5:8], refs[8:11]
    w_out, m_in, v_in = refs[11:14], refs[14:17], refs[17:20]
    w_in = refs[20:23]
    load_sem, r_send, r_recv, d_send, d_recv = refs[23:]
    chips, half = n // 2, n // 4
    me, z, c, partner, plus, minus = places(n)
    per_layer = grads.shape[0] // layers
    pieces = [(layer, i) for layer in range(layers) for i in range(3)]

    def own(ref, layer, i):
        rows = m_in[i].shape[1]
        return ref.at[layer, pl.ds(pl.multiple_of(me * rows, 8), rows), :]

    loads = []
    for p, (layer, i) in enumerate(pieces):
        loads.append(
            [
                pltpu.make_async_copy(own(w_h[i], layer, i), w_in[i].at[layer], load_sem.at[p, 0]),
                pltpu.make_async_copy(m_h[i].at[layer], m_in[i].at[layer], load_sem.at[p, 1]),
                pltpu.make_async_copy(v_h[i].at[layer], v_in[i].at[layer], load_sem.at[p, 2]),
            ]
        )
        for one in loads[-1]:
            one.start()
    greet([partner, plus, minus])
    factor = jnp.minimum(1.0, 0.5 * lax.rsqrt(jnp.sum(square[...]) / count + 1e-30))

    def step(w, m, v, g):
        g = g.astype(F32) * factor
        m = 0.9 * m + 0.1 * g
        v = 0.95 * v + 0.05 * g * g
        w = w.astype(F32)
        return (w - 0.02 * (m * lax.rsqrt(v + 1e-8) + 0.1 * w)).astype(BF), m, v

    def block(ref, p, chip, core, part=None):
        layer, i = pieces[p]
        rows, cols = m_in[i].shape[1:]
        start = (chip * 2 + core) * rows
        if part is None:
            return ref.at[layer, pl.ds(pl.multiple_of(start, 8), rows), :]
        if i == 2:
            return ref.at[layer, pl.ds(pl.multiple_of(start + part * (rows // 2), 8), rows // 2), :]
        return ref.at[layer, pl.ds(pl.multiple_of(start, 8), rows), pl.ds(part * (cols // 2), cols // 2)]

    def part_of(ref, p, part):
        layer, i = pieces[p]
        rows, cols = m_in[i].shape[1:]
        if i == 2:
            return ref.at[layer, pl.ds(part * (rows // 2), rows // 2), :]
        return ref.at[layer, :, pl.ds(part * (cols // 2), cols // 2)]

    def hop(way, s, p):
        i = pieces[p][1]
        chip = lax.rem(z + (chips - s if way == 0 else s), chips)
        part = way if s == half - 1 else None
        dst = block(w_out[i], p, chip, c, part)
        if s == 0:
            src = w_in[i].at[pieces[p][0]] if part is None else part_of(w_in[i], p, part)
        else:
            src = dst
        return pltpu.make_async_remote_copy(
            src_ref=src,
            dst_ref=dst,
            send_sem=r_send.at[way, s, p],
            recv_sem=r_recv.at[way, s, p],
            device_id={"dp": plus if way == 0 else minus},
            device_id_type=MESH,
        )

    def across(j, p):
        i = pieces[p][1]
        if j == 0:
            src, dst = w_in[i].at[pieces[p][0]], block(w_out[i], p, z, c)
        else:
            s, way = (j - 1) // 2, (j - 1) % 2
            chip = lax.rem(z + (chips - 1 - s if way == 0 else 1 + s), chips)
            dst = block(w_out[i], p, chip, c, way if s == half - 1 else None)
            src = dst
        return pltpu.make_async_remote_copy(
            src_ref=src,
            dst_ref=dst,
            send_sem=d_send.at[j, p],
            recv_sem=d_recv.at[j, p],
            device_id={"dp": partner},
            device_id_type=MESH,
        )

    for p, (layer, i) in enumerate(pieces):
        for one in loads[p]:
            one.wait()
        base = (layers - 1 - layer) * per_layer
        rows, cols = m_in[i].shape[1:]
        w1, m1, v1 = w_in[i], m_in[i], v_in[i]
        if i < 2:

            def column(q, _, base=base, layer=layer, i=i, w1=w1, m1=m1, v1=v1):
                t, r = q // QUARTERS, lax.rem(q, QUARTERS)
                at_cols = pl.ds(pl.multiple_of(q * LANES, LANES), LANES)
                g = grads[base + 2 * t + i, r // 2, lax.rem(r, 2)]
                w, m, v = step(w1[layer, :, at_cols], m1[layer, :, at_cols], v1[layer, :, at_cols], g)
                w1[layer, :, at_cols] = w
                m1[layer, :, at_cols] = m
                v1[layer, :, at_cols] = v
                return 0

            lax.fori_loop(0, cols // LANES, column, 0, unroll=5)
        else:

            def row(j, _, base=base, layer=layer, w1=w1, m1=m1, v1=v1):
                at_rows = pl.ds(pl.multiple_of(j * 32, 32), 32)
                g = grads[base + 2 * tiles + j].astype(F32)
                eights = [g[r // 2, r % 2] for r in range(4)]
                g = jnp.concatenate(
                    [jnp.concatenate([e[8 * q : 8 * q + 8, :] for q in range(cols // LANES)], axis=1) for e in eights], axis=0
                )
                w, m, v = step(w1[layer, at_rows, :], m1[layer, at_rows, :], v1[layer, at_rows, :], g)
                w1[layer, at_rows, :] = w
                m1[layer, at_rows, :] = m
                v1[layer, at_rows, :] = v
                return 0

            lax.fori_loop(0, rows // 32, row, 0, unroll=5)
        if p == 0:
            meet(3)
        for way in (0, 1):
            hop(way, 0, p).start()
        across(0, p).start()
        start = pl.ds(pl.multiple_of(me * rows, 8), rows)
        w_out[i][layer, start, :] = w1[layer]
    for s in range(1, half + 1):
        for p in range(len(pieces)):
            for way in (0, 1):
                hop(way, s - 1, p).wait_recv()
                if s < half:
                    hop(way, s, p).start()
                across(1 + 2 * (s - 1) + way, p).start()
    for p in range(len(pieces)):
        for j in range(1 + 2 * half):
            across(j, p).wait()
        for s in range(half):
            for way in (0, 1):
                hop(way, s, p).wait_send()


def update(n, grads, square, ws, ms, vs):
    layers, d, ff = ws[0].shape
    half = n // 4
    pieces = 3 * layers
    tiles = ff // TILE
    hbm, vmem = pl.BlockSpec(memory_space=pl.ANY), pl.BlockSpec(memory_space=pltpu.VMEM)
    count = sum(w.size for w in ws)
    like = lambda t, dt=None: jax.ShapeDtypeStruct(t.shape, dt or t.dtype)
    return pl.pallas_call(
        functools.partial(update_kernel, n, layers, tiles, count),
        in_specs=[vmem, vmem] + [hbm] * 9,
        out_specs=[vmem] * 9,
        out_shape=[pltpu.VMEM(t.shape, t.dtype) for t in (*ws, *ms, *vs)],
        scratch_shapes=[pltpu.VMEM(m.shape, BF) for m in ms]
        + [
            pltpu.SemaphoreType.DMA((pieces, 3)),
            pltpu.SemaphoreType.DMA((2, half, pieces)),
            pltpu.SemaphoreType.DMA((2, half, pieces)),
            pltpu.SemaphoreType.DMA((1 + 2 * half, pieces)),
            pltpu.SemaphoreType.DMA((1 + 2 * half, pieces)),
        ],
        compiler_params=pltpu.CompilerParams(collective_id=1, has_side_effects=True, vmem_limit_bytes=4_000_000),
        name="update",
    )(
        *(pltpu.with_memory_space_constraint(t, pltpu.VMEM) for t in (grads, square)),
        *(pltpu.with_memory_space_constraint(t, pltpu.HBM) for t in (*ws, *ms, *vs)),
    )


def place_kernel(*refs):
    k = len(refs) // 2
    sems = refs[-1]
    copies = [pltpu.make_async_copy(refs[i], refs[k + i], sems.at[i]) for i in range(k)]
    for one in copies:
        one.start()
    for one in copies:
        one.wait()


def place(arrays):
    hbm, vmem = pl.BlockSpec(memory_space=pl.ANY), pl.BlockSpec(memory_space=pltpu.VMEM)
    return pl.pallas_call(
        place_kernel,
        in_specs=[vmem] * len(arrays),
        out_specs=[hbm] * len(arrays),
        out_shape=[pltpu.HBM(t.shape, t.dtype) for t in arrays],
        scratch_shapes=[pltpu.SemaphoreType.DMA((len(arrays),))],
        compiler_params=pltpu.CompilerParams(vmem_limit_bytes=1_000_000),
        name="place",
    )(*(pltpu.with_memory_space_constraint(t, pltpu.VMEM) for t in arrays))


def solution(mesh):
    n = mesh.shape["dp"]

    def of_a_device(x, dy, *arrays):
        ws, ms, vs = (arrays[i : i + 3] for i in (0, 3, 6))
        grads, square = backward(n, x[0], dy[0], *ws)
        return tuple(place(update(n, grads, square, ws, ms, vs)))

    seq, whole, rows = P(("rep", "dp")), P(), P(None, "dp")
    return jax.shard_map(
        of_a_device,
        mesh=mesh,
        in_specs=(seq, seq) + (whole,) * 3 + (rows,) * 6,
        out_specs=(P("rep"),) * 3 + (P("rep", "dp"),) * 6,
        check_vma=False,
    )
```

time: 420 us -> 356 us (0.85)
  local copies, waits for them, and re-layouts: 44.6 us -> 0 us
  Pallas kernels: 374 us -> 355 us
    unnamed x35 -> x0, local copies, waits for them, and re-layouts: 44.6 us -> none
    pallas_call x1, Pallas kernels: 27.1 us -> 11.4 us  [place(): pl.pallas_call(place_kernel, in_specs=[vmem] * len(arrays), out_specs=[hb...]
    pallas_call x1, Pallas kernels: 151 us -> 137 us  [update(): pl.pallas_call(functools.partial(update_kernel, n, layers, tiles, count),...]
    pallas_call x1, Pallas kernels: 196 us -> 206 us  [backward(): pl.pallas_call(functools.partial(backward_kernel, n, layers, tiles, rows)...]
where the time goes in v3:
time: 356 us
  Pallas kernels  355 us (100%)
    pallas_call x1, Pallas kernels, backward(): pl.pallas_call(functools.partial(backward_kernel, n, layers, tiles, rows)...  206 us
    pallas_call x1, Pallas kernels, update(): pl.pallas_call(functools.partial(update_kernel, n, layers, tiles, count),...  137 us
    pallas_call x1, Pallas kernels, place(): pl.pallas_call(place_kernel, in_specs=[vmem] * len(arrays), out_specs=[hb...  11.4 us

profile of v3, /device:TPU:21, one launch (start us, length us, event | category | flops | bytes accessed | tf_op | source)
XLA Modules:
  0.0 355.9 jit_solution(8203778847234250517)
XLA Ops:
  0.6 206.5 %backward.1 = (bf16[30,2,2,56,128]{4,3,2,1,0:T(8,128)(2,1)S(1)}, f32[8,128]{1,0:T(8,128)S(1)}) custom-call(bf16[1024,896]{1,0:T(8,128)(2,1)} %bitcast.2, bf16[1024,896]{1,0:T(8,128)(2,1)} %bitcast.3, bf16[2,896,2560]{2,1,0:T(8,128)(2,1)} %refs_2_.1, bf16[2,896,2560]{2,1,0:T(8,128)(2,1)} %refs_3_.1, bf16[2,2560,896]{2,1,0:T(8,128)(2,1)} %refs_4_.1), custom_call_target="tpu_custom_call" | custom-call | tf_op jit(solution)/shard_map/backward/pallas_call | solution.py:390
  207.1 137.2 %update.1 = (bf16[2,896,2560]{2,1,0:T(8,128)(2,1)S(1)}, bf16[2,896,2560]{2,1,0:T(8,128)(2,1)S(1)}, bf16[2,2560,896]{2,1,0:T(8,128)(2,1)S(1)}, f32[2,56,2560]{2,1...) custom-call(bf16[30,2,2,56,128]{4,3,2,1,0:T(8,128)(2,1)S(1)} %get-tu, ...), custom_call_target="tpu_custom_call" | custom-call | tf_op jit(solution)/shard_map/update/pallas_call | solution.py:583
  344.3 11.4 %place.1 = (bf16[2,896,2560]{2,1,0:T(8,128)(2,1)}, bf16[2,896,2560]{2,1,0:T(8,128)(2,1)}, bf16[2,2560,896]{2,1,0:T(8,128)(2,1)}, f32[2,56,2560]{2,1,0:T(8,128)},...) custom-call(bf16[2,896,2560]{2,1,0:T(8,128)(2,1)S(1)} %get-tuple-ele, ...), custom_call_target="tpu_custom_call" | custom-call | tf_op jit(solution)/shard_map/place/pallas_call | solution.py:616

commit v4 on v3

--- a/solution.py
+++ b/solution.py
@@ -16,7 +16,7 @@
 LAG = 2
 LAG_PARTNER = 1
 RING_GRAD, RING_SUM, RING_PARTNER = 4, 10, 4
-VMEM_LIMIT = 62_000_000
+VMEM_LIMIT = 63_500_000
 
 
 def nn(a, b):
@@ -61,10 +61,10 @@
 
 def backward_kernel(
     n, layers, tiles, rows,
-    x_h, dy_h, wg_h, wu_h, wd_h,
-    out, square,
+    x_h, dy_h, wg_h, wu_h, wd_h, m_h, v_h,
+    out, square, w_first, m_first, v_first,
     h, a0, a1, at, dy, wg, wu, wd, act, dgate, dup, acc,
-    grad, partner_sum, total, hop_in, squares, everyone,
+    grad, partner_sum, total, hop_out, hop_in, squares, everyone,
     d_send, d_recv, r_send, r_recv, s_send, s_recv, load_sem, wide_sem, tall_sem,
 ):
     chips, half = n // 2, n // 4
@@ -121,17 +121,21 @@
     load_x.start()
     start(wide_weights(0, jnp.int32(0)))
     tall_weights(0, jnp.int32(0), jnp.int32(0)).start()
-    for t in range(1, tiles):
-        start(wide_weights(0, jnp.int32(t)))
-    load_dy.start()
-    others = [lax.rem(me + i, n) for i in range(1, n)]
+    own_rows = pl.ds(pl.multiple_of(me * rows, 8), rows)
+    first = [
+        pltpu.make_async_copy(wg_h.at[0, own_rows, :], w_first, load_sem.at[2]),
+        pltpu.make_async_copy(m_h.at[0], m_first, load_sem.at[3]),
+        pltpu.make_async_copy(v_h.at[0], v_first, load_sem.at[4]),
+    ]
+    steps_away = sorted(range(1, n), key=lambda i: -min(i, n - i))
+    others = [lax.rem(me + i, n) for i in steps_away]
     greet(others)
     squares[...] = jnp.zeros_like(squares)
     acc[...] = jnp.zeros_like(acc)
 
     def place_of(k):
         within = lax.rem(k, per_layer)
-        tall = within // (2 * tiles)
+        tall = lax.div(within, 2 * tiles)
         return tall * (within - 2 * tiles + RING_GRAD) + (1 - tall) * lax.rem(within, RING_GRAD)
 
     def to_partner(k):
@@ -148,93 +152,146 @@
     def target(way, s):
         return lax.rem(z + (half - s if way == 0 else chips - half + s), chips)
 
-    def hop(way, s, slot):
-        k = lax.rem(slot - LAG_PARTNER - LAG * s, RING_SUM)
-        b = lax.rem(slot, slots)
-        src, dst = total.at[k, target(way, s)], hop_in.at[way, s, b]
-        if s == 0:
-            src, dst = src.at[way], dst.at[way]
+    def hop(way, slot, low=0, high=half - 1):
+        out_b, in_b = lax.rem(slot, LAG), lax.rem(slot, slots)
+        part = pl.ds(max(2 * low - 1, 0), 2 * high + 1 - max(2 * low - 1, 0))
         return pltpu.make_async_remote_copy(
-            src_ref=src,
-            dst_ref=dst,
-            send_sem=r_send.at[way, s, b],
-            recv_sem=r_recv.at[way, s, b],
+            src_ref=hop_out.at[way, out_b, part],
+            dst_ref=hop_in.at[way, in_b, part],
+            send_sem=r_send.at[way, out_b],
+            recv_sem=r_recv.at[way, in_b],
             device_id={"dp": plus if way == 0 else minus},
             device_id_type=MESH,
         )
+
+    def first_step(k, now):
+        i, b = place_of(k), lax.rem(k, RING_PARTNER)
+        for way in (0, 1):
+            far = target(way, 0)
+            own, other = grad[i, c, far, way].astype(F32), partner_sum[b, far, way].astype(F32)
+            hop_out[way, lax.rem(now, LAG), 0] = (own + other).astype(BF)
+
+    def next_step(s, k, now):
+        i, b = lax.rem(k, RING_SUM), lax.rem(now - LAG, slots)
+        for way in (0, 1):
+            far, to = target(way, s), hop_out.at[way, lax.rem(now, LAG)]
+            for h in (0, 1):
+                own = total[i, far, h]
+                if s > 1:
+                    own = (own.astype(F32) + hop_in[way, b, 2 * s - 3 + h].astype(F32)).astype(BF)
+                elif h == way:
+                    own = (own.astype(F32) + hop_in[way, b, 0].astype(F32)).astype(BF)
+                to[2 * s - 1 + h] = own
 
     def add_partner(k):
         i, g, b = lax.rem(k, RING_SUM), place_of(k), lax.rem(k, RING_PARTNER)
         for j in range(chips):
             total[i, j] = (grad[g, c, j].astype(F32) + partner_sum[b, j].astype(F32)).astype(BF)
 
-    def add_hop(way, s, k, now):
-        i, b, far = lax.rem(k, RING_SUM), lax.rem(now - LAG, slots), target(way, s)
-        if s == 1:
-            total[i, far, way] = (total[i, far, way].astype(F32) + hop_in[way, 0, b, way].astype(F32)).astype(BF)
-        else:
-            total[i, far] = (total[i, far].astype(F32) + hop_in[way, s - 1, b].astype(F32)).astype(BF)
-
     def finish(k, now):
-        b = lax.rem(now - LAG, slots)
-        own = total[lax.rem(k, RING_SUM), z].astype(F32)
-        g = (own + hop_in[0, half - 1, b].astype(F32) + hop_in[1, half - 1, b].astype(F32)).astype(BF)
-        out[k] = g
-        wide = g.astype(F32)
-        squares[...] += wide[0, 0] * wide[0, 0] + wide[0, 1] * wide[0, 1] + wide[1, 0] * wide[1, 0] + wide[1, 1] * wide[1, 1]
+        i, b = lax.rem(k, RING_SUM), lax.rem(now - LAG, slots)
+        squared = []
+        for h in (0, 1):
+            at_end = 2 * half - 3 + h
+            g = total[i, z, h].astype(F32) + hop_in[0, b, at_end].astype(F32) + hop_in[1, b, at_end].astype(F32)
+            out[k, h] = g.astype(BF)
+            wide = out[k, h].astype(F32)
+            squared.append(wide[0] * wide[0] + wide[1] * wide[1])
+        squares[...] += squared[0] + squared[1]
+
+    def steps(now):
+        return [now - LAG_PARTNER - LAG * s for s in range(half + 1)]
 
     def slot(now):
-        ks = [now - LAG_PARTNER - LAG * s for s in range(half + 1)]
-        filled = (ks[half] >= 0) & (now < chunks)
-
-        @pl.when(filled)
+        ks = steps(now)
+        to_partner(now).start()
+        to_partner(ks[0]).wait()
+        for way in (0, 1):
+            hop(way, now - LAG).wait()
+        first_step(ks[0], now)
+        for s in range(1, half):
+            next_step(s, ks[s], now)
+        finish(ks[half], now)
+        for way in (0, 1):
+            hop(way, now).start()
+        add_partner(ks[0])
+
+    def filling(now):
+        ks = steps(now)
+
+        @pl.when(now >= 0)
         def _():
             to_partner(now).start()
+
+        for high in range(half):
+
+            @pl.when((ks[high] >= LAG) & (ks[high] < 2 * LAG) if high < half - 1 else ks[high] >= LAG)
+            def _(high=high):
+                for way in (0, 1):
+                    hop(way, now - LAG, 0, high).wait()
+
+        @pl.when(ks[0] >= 0)
+        def _():
             to_partner(ks[0]).wait()
-            for s in range(1, half + 1):
+            first_step(ks[0], now)
+
+        for s in range(1, half):
+
+            @pl.when(ks[s] >= 0)
+            def _(s=s):
+                next_step(s, ks[s], now)
+
+        @pl.when(ks[half] >= 0)
+        def _():
+            finish(ks[half], now)
+
+        for high in range(half):
+
+            @pl.when((ks[high] >= 0) & (ks[high] < LAG) if high < half - 1 else ks[high] >= 0)
+            def _(high=high):
                 for way in (0, 1):
-                    hop(way, s - 1, now - LAG).wait()
+                    hop(way, now, 0, high).start()
+
+        @pl.when(ks[0] >= 0)
+        def _():
             add_partner(ks[0])
-            for s in range(1, half):
+
+    def emptying(now):
+        ks = steps(now)
+        left = [k < chunks for k in ks]
+
+        def only(low, k):
+            return (k - LAG * low < chunks) & (k - LAG * low >= chunks - LAG) if low > 0 else k < chunks
+
+        for low in range(half):
+
+            @pl.when(only(low, ks[0] - LAG))
+            def _(low=low):
                 for way in (0, 1):
-                    add_hop(way, s, ks[s], now)
-            finish(ks[half], now)
-            for s in range(half):
+                    hop(way, now - LAG, low).wait()
+
+        @pl.when(left[0])
+        def _():
+            to_partner(ks[0]).wait()
+            first_step(ks[0], now)
+
+        for s in range(1, half):
+
+            @pl.when(left[s])
+            def _(s=s):
+                next_step(s, ks[s], now)
+
+        finish(ks[half], now)
+        for low in range(half):
+
+            @pl.when(only(low, ks[0]))
+            def _(low=low):
                 for way in (0, 1):
-                    hop(way, s, now).start()
-
-        @pl.when(jnp.logical_not(filled))
+                    hop(way, now, low).start()
+
+        @pl.when(left[0])
         def _():
-            def during(k):
-                return (k >= 0) & (k < chunks)
-
-            @pl.when(during(now))
-            def _():
-                to_partner(now).start()
-
-            @pl.when(during(ks[0]))
-            def _():
-                to_partner(ks[0]).wait()
-                add_partner(ks[0])
-
-            for s in range(1, half + 1):
-
-                @pl.when(during(ks[s]))
-                def _(s=s):
-                    for way in (0, 1):
-                        hop(way, s - 1, now - LAG).wait()
-                    if s < half:
-                        for way in (0, 1):
-                            add_hop(way, s, ks[s], now)
-                    else:
-                        finish(ks[s], now)
-
-            for s in range(half):
-
-                @pl.when(during(ks[s]))
-                def _(s=s):
-                    for way in (0, 1):
-                        hop(way, s, now).start()
+            add_partner(ks[0])
 
     def forward(b, a, t):
         for r in range(0, tokens, ROWS):
@@ -266,20 +323,24 @@
                     grad[k, dev % 2, dev // 2, q // 2, q % 2] = g[i * rows : (i + 1) * rows, q * LANES : (q + 1) * LANES].astype(BF)
 
     def tall_grad(t):
+        per_dev = tiles * TILE // n // 8
+        first_dev, first_rest = lax.div(t * (TILE // 8), per_dev), lax.rem(t * (TILE // 8), per_dev)
+
+        def put(i, eight):
+            rest = first_rest + i
+            over = sum(jnp.where(rest >= per_dev * m, 1, 0) for m in range(1, TILE // 8 // per_dev + 2))
+            dev, rest = first_dev + over, rest - per_dev * over
+            k, quarter = RING_GRAD + (rest >> 2), rest & 3
+            stacked = jnp.concatenate([eight[:, q * LANES : (q + 1) * LANES] for q in range(d // LANES)], axis=0)
+            grad[k, dev & 1, dev >> 1, quarter >> 1, quarter & 1] = stacked.astype(BF)
+
         acc[:TILE, :] = tn(act[t], dy[...])
-        per_dev = tiles * TILE // n // 8
 
         def group(i, _):
-            g = t * (TILE // 8) + i
-            dev, rest = g // per_dev, lax.rem(g, per_dev)
-            k = RING_GRAD + rest // 4
-            eight = acc[pl.ds(pl.multiple_of(i * 8, 8), 8), :]
-            stacked = jnp.concatenate([eight[:, q * LANES : (q + 1) * LANES] for q in range(d // LANES)], axis=0)
-            quarter = lax.rem(rest, 4)
-            grad[k, lax.rem(dev, 2), dev // 2, quarter // 2, lax.rem(quarter, 2)] = stacked.astype(BF)
+            put(i, acc[pl.ds(pl.multiple_of(i * 8, 8), 8), :])
             return 0
 
-        lax.fori_loop(0, TILE // 8, group, 0, unroll=8)
+        lax.fori_loop(0, TILE // 8, group, 0, unroll=16)
 
     def to_states(layer, a, first_slot):
         turn = 0
@@ -293,14 +354,15 @@
                     a[at_rows, :] = part.astype(BF)
                 else:
                     acc[at_rows, :] = part
-                slot(first_slot + turn)
-                turn += 1
+                if turn < 3:
+                    slot(first_slot + turn)
+                    turn += 1
             which = 0 if source is dgate else 1
             for t in range(tiles):
                 wide_weight(which, layer - 1, jnp.int32(t)).start()
 
         def norm(i, _):
-            at_rows = pl.ds(pl.multiple_of(i * 64, 64), 64)
+            at_rows = pl.ds(pl.multiple_of(i * 32, 32), 32)
             by_a = (a[at_rows, :].astype(F32) + acc[at_rows, :].astype(BF).astype(F32)).astype(BF).astype(F32)
             wide = h[at_rows, :].astype(F32)
             scale = lax.rsqrt(jnp.mean(wide * wide, -1, keepdims=True) + 1e-6)
@@ -309,10 +371,14 @@
             dy[at_rows, :] = (dy[at_rows, :].astype(F32) + by_h.astype(F32)).astype(BF)
             return 0
 
-        lax.fori_loop(0, tokens // 64, norm, 0)
+        lax.fori_loop(0, tokens // 32, norm, 0, unroll=4)
         slot(first_slot + turn)
 
     load_x.wait()
+    for t in range(1, tiles):
+        start(wide_weights(0, jnp.int32(t)))
+    load_dy.start()
+    start(first)
     for r in range(0, tokens, 128):
         a0[r : r + 128, :] = normed(h[r : r + 128, :])
 
@@ -323,12 +389,14 @@
         start(wide_weights(layers - 1, t))
 
     each_tile(ahead)
+
     for r in range(0, tokens, 128):
         new = (h[r : r + 128, :].astype(F32) + acc[r : r + 128, :].astype(BF).astype(F32)).astype(BF)
         h[r : r + 128, :] = new
         a1[r : r + 128, :] = normed(new)
     at[...] = a1[...].T
     load_dy.wait()
+    wait(first)
     meet(n - 1)
 
     for step in range(layers):
@@ -342,22 +410,45 @@
             next_tall(layer, t, turn, layer - 1 if layer > 0 else None)
             chunk = base + 2 * t
             elementwise(lax.rem(turn, 2), a, t)
-            slot(chunk - 1)
             wide_grad(dgate, chunk, t)
-            slot(chunk)
-            wide_grad(dup, chunk + 1, t)
-            tall_grad(t)
+            if step == 0:
+                filling(chunk)
+                wide_grad(dup, chunk + 1, t)
+
+                @pl.when(t + 1 < tiles)
+                def _():
+                    filling(chunk + 1)
+
+            else:
+                slot(chunk)
+                wide_grad(dup, chunk + 1, t)
+                tall_grad(t)
+                slot(chunk + 1)
 
         each_tile(tile)
-        if step < layers - 1:
-            to_states(layer, a, base + 2 * tiles - 1)
+        if step == 0:
+
+            def down(t, base=base):
+                tall_grad(t)
+
+                @pl.when(t == 1)
+                def _():
+                    slot(base + 2 * tiles - 1)
+
+            each_tile(down)
+            slot(base + 2 * tiles)
+            to_states(layer, a, base + 2 * tiles + 1)
             at[...] = a0[...].T
 
-    def rest(i, _):
-        slot(i)
-        return 0
-
-    lax.fori_loop((layers - 1) * per_layer + 2 * tiles - 1, chunks + full, rest, 0)
+    def rest(turn_of):
+        def body(i, _):
+            turn_of(i)
+            return 0
+
+        return body
+
+    lax.fori_loop((layers - 1) * per_layer + 2 * tiles, chunks, rest(slot), 0)
+    lax.fori_loop(chunks, chunks + full, rest(emptying), 0)
 
     everyone[me] = jnp.sum(squares[...].reshape(-1, 8, LANES), axis=0)
 
@@ -374,13 +465,13 @@
     for i in range(n - 1):
         share(i, me).start()
     for i in range(n - 1):
-        share(i, lax.rem(me + n - 1 - i, n)).wait_recv()
+        share(i, lax.rem(me + n - steps_away[i], n)).wait_recv()
     square[...] = jnp.sum(everyone[...], axis=0)
     for i in range(n - 1):
         share(i, me).wait_send()
 
 
-def backward(n, x, dy, wg, wu, wd):
+def backward(n, x, dy, wg, wu, wd, m, v):
     layers, d, ff = wg.shape
     tokens = dy.shape[0]
     tiles, rows, chips, half = ff // TILE, d // n, n // 2, n // 4
@@ -389,9 +480,10 @@
     hbm, vmem = pl.BlockSpec(memory_space=pl.ANY), pl.BlockSpec(memory_space=pltpu.VMEM)
     return pl.pallas_call(
         functools.partial(backward_kernel, n, layers, tiles, rows),
-        in_specs=[hbm] * 5,
-        out_specs=[vmem] * 2,
-        out_shape=[pltpu.VMEM((chunks,) + unit, BF), pltpu.VMEM((8, LANES), F32)],
+        in_specs=[hbm] * 7,
+        out_specs=[vmem] * 5,
+        out_shape=[pltpu.VMEM((chunks,) + unit, BF), pltpu.VMEM((8, LANES), F32)]
+        + [pltpu.VMEM((rows, ff), dt) for dt in (BF, F32, F32)],
         scratch_shapes=[
             pltpu.VMEM((tokens, d), BF),
             pltpu.VMEM((tokens, d), BF),
@@ -408,30 +500,32 @@
             pltpu.VMEM((RING_GRAD + tiles, 2, chips) + unit, BF),
             pltpu.VMEM((RING_PARTNER, chips) + unit, BF),
             pltpu.VMEM((RING_SUM, chips) + unit, BF),
-            pltpu.VMEM((2, half, 2 * LAG) + unit, BF),
+            pltpu.VMEM((2, LAG, 2 * half - 1) + unit[1:], BF),
+            pltpu.VMEM((2, 2 * LAG, 2 * half - 1) + unit[1:], BF),
             pltpu.VMEM((rows, LANES), F32),
             pltpu.VMEM((n, 8, LANES), F32),
             pltpu.SemaphoreType.DMA((RING_PARTNER,)),
             pltpu.SemaphoreType.DMA((RING_PARTNER,)),
-            pltpu.SemaphoreType.DMA((2, half, 2 * LAG)),
-            pltpu.SemaphoreType.DMA((2, half, 2 * LAG)),
+            pltpu.SemaphoreType.DMA((2, LAG)),
+            pltpu.SemaphoreType.DMA((2, 2 * LAG)),
             pltpu.SemaphoreType.DMA((n - 1,)),
             pltpu.SemaphoreType.DMA((n - 1,)),
-            pltpu.SemaphoreType.DMA((2,)),
+            pltpu.SemaphoreType.DMA((5,)),
             pltpu.SemaphoreType.DMA((2, tiles)),
             pltpu.SemaphoreType.DMA((2,)),
         ],
         compiler_params=pltpu.CompilerParams(collective_id=0, has_side_effects=True, vmem_limit_bytes=VMEM_LIMIT),
         name="backward",
-    )(x, dy, wg, wu, wd)
+    )(x, dy, wg, wu, wd, m, v)
 
 
 def update_kernel(n, layers, tiles, count, *refs):
     grads, square = refs[:2]
-    w_h, m_h, v_h = refs[2:5], refs[5:8], refs[8:11]
-    w_out, m_in, v_in = refs[11:14], refs[14:17], refs[17:20]
-    w_in = refs[20:23]
-    load_sem, r_send, r_recv, d_send, d_recv = refs[23:]
+    first = refs[2:5]
+    w_h, m_h, v_h = refs[5:8], refs[8:11], refs[11:14]
+    w_out, m_in, v_in = refs[14:17], refs[17:20], refs[20:23]
+    w_in = refs[23:26]
+    load_sem, r_send, r_recv, d_send, d_recv = refs[26:]
     chips, half = n // 2, n // 4
     me, z, c, partner, plus, minus = places(n)
     per_layer = grads.shape[0] // layers
@@ -441,8 +535,11 @@
         rows = m_in[i].shape[1]
         return ref.at[layer, pl.ds(pl.multiple_of(me * rows, 8), rows), :]
 
-    loads = []
+    greet([partner, plus, minus])
+    loads = [[]]
     for p, (layer, i) in enumerate(pieces):
+        if p == 0:
+            continue
         loads.append(
             [
                 pltpu.make_async_copy(own(w_h[i], layer, i), w_in[i].at[layer], load_sem.at[p, 0]),
@@ -452,7 +549,6 @@
         )
         for one in loads[-1]:
             one.start()
-    greet([partner, plus, minus])
     factor = jnp.minimum(1.0, 0.5 * lax.rsqrt(jnp.sum(square[...]) / count + 1e-30))
 
     def step(w, m, v, g):
@@ -523,11 +619,12 @@
         w1, m1, v1 = w_in[i], m_in[i], v_in[i]
         if i < 2:
 
-            def column(q, _, base=base, layer=layer, i=i, w1=w1, m1=m1, v1=v1):
+            def column(q, _, base=base, layer=layer, i=i, w1=w1, m1=m1, v1=v1, p=p):
                 t, r = q // QUARTERS, lax.rem(q, QUARTERS)
                 at_cols = pl.ds(pl.multiple_of(q * LANES, LANES), LANES)
                 g = grads[base + 2 * t + i, r // 2, lax.rem(r, 2)]
-                w, m, v = step(w1[layer, :, at_cols], m1[layer, :, at_cols], v1[layer, :, at_cols], g)
+                old = [one[:, at_cols] for one in first] if p == 0 else [one[layer, :, at_cols] for one in (w1, m1, v1)]
+                w, m, v = step(*old, g)
                 w1[layer, :, at_cols] = w
                 m1[layer, :, at_cols] = m
                 v1[layer, :, at_cols] = v
@@ -557,22 +654,27 @@
         across(0, p).start()
         start = pl.ds(pl.multiple_of(me * rows, 8), rows)
         w_out[i][layer, start, :] = w1[layer]
+    def settle(s, p):
+        for way in (0, 1):
+            hop(way, s, p).wait_send()
+            across(1 + 2 * s + way, p).wait()
+
     for s in range(1, half + 1):
         for p in range(len(pieces)):
+            if s == half:
+                across(0, p).wait()
+                for early in range(half - 1):
+                    settle(early, p)
             for way in (0, 1):
                 hop(way, s - 1, p).wait_recv()
                 if s < half:
                     hop(way, s, p).start()
                 across(1 + 2 * (s - 1) + way, p).start()
     for p in range(len(pieces)):
-        for j in range(1 + 2 * half):
-            across(j, p).wait()
-        for s in range(half):
-            for way in (0, 1):
-                hop(way, s, p).wait_send()
-
-
-def update(n, grads, square, ws, ms, vs):
+        settle(half - 1, p)
+
+
+def update(n, grads, square, first, ws, ms, vs):
     layers, d, ff = ws[0].shape
     half = n // 4
     pieces = 3 * layers
@@ -582,7 +684,7 @@
     like = lambda t, dt=None: jax.ShapeDtypeStruct(t.shape, dt or t.dtype)
     return pl.pallas_call(
         functools.partial(update_kernel, n, layers, tiles, count),
-        in_specs=[vmem, vmem] + [hbm] * 9,
+        in_specs=[vmem] * 5 + [hbm] * 9,
         out_specs=[vmem] * 9,
         out_shape=[pltpu.VMEM(t.shape, t.dtype) for t in (*ws, *ms, *vs)],
         scratch_shapes=[pltpu.VMEM(m.shape, BF) for m in ms]
@@ -596,7 +698,7 @@
         compiler_params=pltpu.CompilerParams(collective_id=1, has_side_effects=True, vmem_limit_bytes=4_000_000),
         name="update",
     )(
-        *(pltpu.with_memory_space_constraint(t, pltpu.VMEM) for t in (grads, square)),
+        *(pltpu.with_memory_space_constraint(t, pltpu.VMEM) for t in (grads, square, *first)),
         *(pltpu.with_memory_space_constraint(t, pltpu.HBM) for t in (*ws, *ms, *vs)),
     )
 
@@ -604,7 +706,8 @@
 def place_kernel(*refs):
     k = len(refs) // 2
     sems = refs[-1]
-    copies = [pltpu.make_async_copy(refs[i], refs[k + i], sems.at[i]) for i in range(k)]
+    layers = refs[0].shape[0]
+    copies = [pltpu.make_async_copy(refs[i].at[j], refs[k + i].at[j], sems.at[i, j]) for j in range(layers) for i in range(k)]
     for one in copies:
         one.start()
     for one in copies:
@@ -618,7 +721,7 @@
         in_specs=[vmem] * len(arrays),
         out_specs=[hbm] * len(arrays),
         out_shape=[pltpu.HBM(t.shape, t.dtype) for t in arrays],
-        scratch_shapes=[pltpu.SemaphoreType.DMA((len(arrays),))],
+        scratch_shapes=[pltpu.SemaphoreType.DMA((len(arrays), arrays[0].shape[0]))],
         compiler_params=pltpu.CompilerParams(vmem_limit_bytes=1_000_000),
         name="place",
     )(*(pltpu.with_memory_space_constraint(t, pltpu.VMEM) for t in arrays))
@@ -629,8 +732,8 @@
 
     def of_a_device(x, dy, *arrays):
         ws, ms, vs = (arrays[i : i + 3] for i in (0, 3, 6))
-        grads, square = backward(n, x[0], dy[0], *ws)
-        return tuple(place(update(n, grads, square, ws, ms, vs)))
+        grads, square, *first = backward(n, x[0], dy[0], *ws, ms[0], vs[0])
+        return tuple(place(update(n, grads, square, first, ws, ms, vs)))
 
     seq, whole, rows = P(("rep", "dp")), P(), P(None, "dp")
     return jax.shard_map(

time: 356 us -> 338 us (0.949)
  Pallas kernels: 355 us -> 337 us
    pallas_call x1, Pallas kernels: 206 us -> 189 us  [backward(): pl.pallas_call(functools.partial(backward_kernel, n, layers, tiles, rows)...]
where the time goes in v4:
time: 338 us
  Pallas kernels  337 us (100%)
    pallas_call x1, Pallas kernels, backward(): pl.pallas_call(functools.partial(backward_kernel, n, layers, tiles, rows)...  189 us
    pallas_call x1, Pallas kernels, update(): pl.pallas_call(functools.partial(update_kernel, n, layers, tiles, count),...  137 us
    pallas_call x1, Pallas kernels, place(): pl.pallas_call(place_kernel, in_specs=[vmem] * len(arrays), out_specs=[hb...  11.3 us

profile of v4, /device:TPU:21, one launch (start us, length us, event | category | flops | bytes accessed | tf_op | source)
XLA Modules:
  0.0 337.7 jit_solution(14953590779184220999)
XLA Ops:
  0.6 189.0 %backward.1 = (bf16[30,2,2,56,128]{4,3,2,1,0:T(8,128)(2,1)S(1)}, f32[8,128]{1,0:T(8,128)S(1)}, bf16[56,2560]{1,0:T(8,128)(2,1)S(1)}, f32[56,2560]{1,0:T(8,128)S(1)}, f32[56,2560]{1,0:T(8,128)S(1)}) custom-call(bf16[1024,896]{1,0:T(8,128)(2,1)} %bitcast.2, bf16[1024,896]{1,0:T(8,128)(2,1)} %bitcast.3, bf16[2,896,2560]{2,1,0:T(8,128)(2,1)} %refs_5_.1, ...), custom_call_target="tpu_custom_call" | custom-call | tf_op jit(solution)/shard_map/backward/pallas_call | solution.py:481
  189.7 136.5 %update.1 = (bf16[2,896,2560]{2,1,0:T(8,128)(2,1)S(1)}, bf16[2,896,2560]{2,1,0:T(8,128)(2,1)S(1)}, bf16[2,2560,896]{2,1,0:T(8,128)(2,1)S(1)}, f32[2,56,2560]{2,1...) custom-call(bf16[30,2,2,56,128]{4,3,2,1,0:T(8,128)(2,1)S(1)} %get-tu, ...), custom_call_target="tpu_custom_call" | custom-call | tf_op jit(solution)/shard_map/update/pallas_call | solution.py:685
  326.2 11.3 %place.1 = (bf16[2,896,2560]{2,1,0:T(8,128)(2,1)}, bf16[2,896,2560]{2,1,0:T(8,128)(2,1)}, bf16[2,2560,896]{2,1,0:T(8,128)(2,1)}, f32[2,56,2560]{2,1,0:T(8,128)},...) custom-call(bf16[2,896,2560]{2,1,0:T(8,128)(2,1)S(1)} %get-tuple-ele, ...), custom_call_target="tpu_custom_call" | custom-call | tf_op jit(solution)/shard_map/place/pallas_call | solution.py:719

commit v5 on v4

--- a/solution.py
+++ b/solution.py
@@ -65,7 +65,7 @@
     out, square, w_first, m_first, v_first,
     h, a0, a1, at, dy, wg, wu, wd, act, dgate, dup, acc,
     grad, partner_sum, total, hop_out, hop_in, squares, everyone,
-    d_send, d_recv, r_send, r_recv, s_send, s_recv, load_sem, wide_sem, tall_sem,
+    d_send, d_recv, r_send, r_recv, s_send, s_recv, x_sem, load_sem, wide_sem, tall_sem,
 ):
     chips, half = n // 2, n // 4
     per_layer = 3 * tiles
@@ -116,9 +116,14 @@
             def _():
                 tall_weights(after, jnp.int32(0), turn + 1).start()
 
-    load_x = pltpu.make_async_copy(x_h, h, load_sem.at[0])
+    parts = 4
+    some = tokens // parts
+    load_x = [pltpu.make_async_copy(x_h.at[pl.ds(i * some, some), :], h.at[pl.ds(i * some, some), :], x_sem.at[i]) for i in range(parts)]
     load_dy = pltpu.make_async_copy(dy_h, dy, load_sem.at[1])
-    load_x.start()
+    start(load_x)
+    steps_away = sorted(range(1, n), key=lambda i: -min(i, n - i))
+    others = [lax.rem(me + i, n) for i in steps_away]
+    greet(others)
     start(wide_weights(0, jnp.int32(0)))
     tall_weights(0, jnp.int32(0), jnp.int32(0)).start()
     own_rows = pl.ds(pl.multiple_of(me * rows, 8), rows)
@@ -127,9 +132,6 @@
         pltpu.make_async_copy(m_h.at[0], m_first, load_sem.at[3]),
         pltpu.make_async_copy(v_h.at[0], v_first, load_sem.at[4]),
     ]
-    steps_away = sorted(range(1, n), key=lambda i: -min(i, n - i))
-    others = [lax.rem(me + i, n) for i in steps_away]
-    greet(others)
     squares[...] = jnp.zeros_like(squares)
     acc[...] = jnp.zeros_like(acc)
 
@@ -294,12 +296,17 @@
             add_partner(ks[0])
 
     def forward(b, a, t):
-        for r in range(0, tokens, ROWS):
+        def hidden(r):
             mine = a[r : r + ROWS, :]
             gate = nn(mine, wg[t])
             up = nn(mine, wu[t])
-            hidden = (gate * sigmoid(gate) * up).astype(BF)
-            acc[r : r + ROWS, :] += nn(hidden, wd[b])
+            return (gate * sigmoid(gate) * up).astype(BF)
+
+        ready = hidden(0)
+        for r in range(0, tokens, ROWS):
+            following = hidden(r + ROWS) if r + ROWS < tokens else None
+            acc[r : r + ROWS, :] += nn(ready, wd[b])
+            ready = following
 
     def elementwise(b, a, t):
         for r in range(0, tokens, ROWS):
@@ -323,24 +330,26 @@
                     grad[k, dev % 2, dev // 2, q // 2, q % 2] = g[i * rows : (i + 1) * rows, q * LANES : (q + 1) * LANES].astype(BF)
 
     def tall_grad(t):
-        per_dev = tiles * TILE // n // 8
-        first_dev, first_rest = lax.div(t * (TILE // 8), per_dev), lax.rem(t * (TILE // 8), per_dev)
-
-        def put(i, eight):
+        acc[pl.ds(pl.multiple_of(lax.rem(t, 2) * TILE, TILE), TILE), :] = tn(act[t], dy[...])
+
+    def tall_place(t):
+        per_dev = tiles * TILE // n // 16
+        first_dev, first_rest = lax.div(t * (TILE // 16), per_dev), lax.rem(t * (TILE // 16), per_dev)
+        offset = lax.rem(t, 2) * TILE
+        for i in range(TILE // 16):
             rest = first_rest + i
-            over = sum(jnp.where(rest >= per_dev * m, 1, 0) for m in range(1, TILE // 8 // per_dev + 2))
+            low, high = i // per_dev, (i + per_dev - 1) // per_dev
+            over = low if low == high else low + jnp.where(rest >= per_dev * high, 1, 0)
             dev, rest = first_dev + over, rest - per_dev * over
-            k, quarter = RING_GRAD + (rest >> 2), rest & 3
-            stacked = jnp.concatenate([eight[:, q * LANES : (q + 1) * LANES] for q in range(d // LANES)], axis=0)
-            grad[k, dev & 1, dev >> 1, quarter >> 1, quarter & 1] = stacked.astype(BF)
-
-        acc[:TILE, :] = tn(act[t], dy[...])
-
-        def group(i, _):
-            put(i, acc[pl.ds(pl.multiple_of(i * 8, 8), 8), :])
-            return 0
-
-        lax.fori_loop(0, TILE // 8, group, 0, unroll=16)
+            to = grad.at[RING_GRAD + (rest >> 1), dev & 1, dev >> 1, rest & 1]
+            for e in (0, 1):
+                eight = acc[pl.ds(pl.multiple_of(offset + 16 * i + 8 * e, 8), 8), :]
+                stacked = jnp.concatenate([eight[:, q * LANES : (q + 1) * LANES] for q in range(d // LANES)], axis=0)
+                to[e] = stacked.astype(BF)
+
+    def tall_turn(t):
+        tall_place(lax.rem(t + tiles - 1, tiles))
+        tall_grad(t)
 
     def to_states(layer, a, first_slot):
         turn = 0
@@ -361,26 +370,25 @@
             for t in range(tiles):
                 wide_weight(which, layer - 1, jnp.int32(t)).start()
 
-        def norm(i, _):
-            at_rows = pl.ds(pl.multiple_of(i * 32, 32), 32)
+        for r in range(0, tokens, 128):
+            at_rows = pl.ds(r, 128)
             by_a = (a[at_rows, :].astype(F32) + acc[at_rows, :].astype(BF).astype(F32)).astype(BF).astype(F32)
             wide = h[at_rows, :].astype(F32)
             scale = lax.rsqrt(jnp.mean(wide * wide, -1, keepdims=True) + 1e-6)
             along = jnp.mean(by_a * wide, -1, keepdims=True)
             by_h = (by_a * scale - wide * (scale * scale * scale * along)).astype(BF)
             dy[at_rows, :] = (dy[at_rows, :].astype(F32) + by_h.astype(F32)).astype(BF)
-            return 0
-
-        lax.fori_loop(0, tokens // 32, norm, 0, unroll=4)
         slot(first_slot + turn)
 
-    load_x.wait()
-    for t in range(1, tiles):
-        start(wide_weights(0, jnp.int32(t)))
-    load_dy.start()
-    start(first)
-    for r in range(0, tokens, 128):
-        a0[r : r + 128, :] = normed(h[r : r + 128, :])
+    for i in range(parts):
+        load_x[i].wait()
+        if i == parts - 1:
+            for t in range(1, tiles):
+                start(wide_weights(0, jnp.int32(t)))
+            load_dy.start()
+            start(first)
+        for r in range(i * some, (i + 1) * some, 128):
+            a0[r : r + 128, :] = normed(h[r : r + 128, :])
 
     def ahead(t):
         wait(wide_weights(0, t))
@@ -393,8 +401,9 @@
     for r in range(0, tokens, 128):
         new = (h[r : r + 128, :].astype(F32) + acc[r : r + 128, :].astype(BF).astype(F32)).astype(BF)
         h[r : r + 128, :] = new
-        a1[r : r + 128, :] = normed(new)
-    at[...] = a1[...].T
+        new = normed(new)
+        a1[r : r + 128, :] = new
+        at[:, r : r + 128] = new.T
     load_dy.wait()
     wait(first)
     meet(n - 1)
@@ -421,21 +430,25 @@
 
             else:
                 slot(chunk)
+                tall_place(lax.rem(t + tiles - 1, tiles))
                 wide_grad(dup, chunk + 1, t)
                 tall_grad(t)
                 slot(chunk + 1)
 
         each_tile(tile)
+        if step > 0:
+            tall_place(jnp.int32(tiles - 1))
         if step == 0:
 
             def down(t, base=base):
-                tall_grad(t)
+                tall_turn(t)
 
                 @pl.when(t == 1)
                 def _():
                     slot(base + 2 * tiles - 1)
 
             each_tile(down)
+            tall_place(jnp.int32(tiles - 1))
             slot(base + 2 * tiles)
             to_states(layer, a, base + 2 * tiles + 1)
             at[...] = a0[...].T
@@ -510,6 +523,7 @@
             pltpu.SemaphoreType.DMA((2, 2 * LAG)),
             pltpu.SemaphoreType.DMA((n - 1,)),
             pltpu.SemaphoreType.DMA((n - 1,)),
+            pltpu.SemaphoreType.DMA((4,)),
             pltpu.SemaphoreType.DMA((5,)),
             pltpu.SemaphoreType.DMA((2, tiles)),
             pltpu.SemaphoreType.DMA((2,)),

time: 338 us -> 333 us (0.985)
  Pallas kernels: 337 us -> 332 us
    pallas_call x1, Pallas kernels: 189 us -> 184 us  [backward(): pl.pallas_call(functools.partial(backward_kernel, n, layers, tiles, rows)...]
where the time goes in v5:
time: 333 us
  Pallas kernels  332 us (100%)
    pallas_call x1, Pallas kernels, backward(): pl.pallas_call(functools.partial(backward_kernel, n, layers, tiles, rows)...  184 us
    pallas_call x1, Pallas kernels, update(): pl.pallas_call(functools.partial(update_kernel, n, layers, tiles, count),...  137 us
    pallas_call x1, Pallas kernels, place(): pl.pallas_call(place_kernel, in_specs=[vmem] * len(arrays), out_specs=[hb...  11.3 us

profile of v5, /device:TPU:21, one launch (start us, length us, event | category | flops | bytes accessed | tf_op | source)
XLA Modules:
  0.0 332.8 jit_solution(13305003461870265039)
XLA Ops:
  0.6 184.1 %backward.1 = (bf16[30,2,2,56,128]{4,3,2,1,0:T(8,128)(2,1)S(1)}, f32[8,128]{1,0:T(8,128)S(1)}, bf16[56,2560]{1,0:T(8,128)(2,1)S(1)}, f32[56,2560]{1,0:T(8,128)S(1)}, f32[56,2560]{1,0:T(8,128)S(1)}) custom-call(bf16[1024,896]{1,0:T(8,128)(2,1)} %bitcast.2, bf16[1024,896]{1,0:T(8,128)(2,1)} %bitcast.3, bf16[2,896,2560]{2,1,0:T(8,128)(2,1)} %refs_5_.1, ...), custom_call_target="tpu_custom_call" | custom-call | tf_op jit(solution)/shard_map/backward/pallas_call | solution.py:494
  184.8 136.5 %update.1 = (bf16[2,896,2560]{2,1,0:T(8,128)(2,1)S(1)}, bf16[2,896,2560]{2,1,0:T(8,128)(2,1)S(1)}, bf16[2,2560,896]{2,1,0:T(8,128)(2,1)S(1)}, f32[2,56,2560]{2,1...) custom-call(bf16[30,2,2,56,128]{4,3,2,1,0:T(8,128)(2,1)S(1)} %get-tu, ...), custom_call_target="tpu_custom_call" | custom-call | tf_op jit(solution)/shard_map/update/pallas_call | solution.py:699
  321.3 11.3 %place.1 = (bf16[2,896,2560]{2,1,0:T(8,128)(2,1)}, bf16[2,896,2560]{2,1,0:T(8,128)(2,1)}, bf16[2,2560,896]{2,1,0:T(8,128)(2,1)}, f32[2,56,2560]{2,1,0:T(8,128)},...) custom-call(bf16[2,896,2560]{2,1,0:T(8,128)(2,1)S(1)} %get-tuple-ele, ...), custom_call_target="tpu_custom_call" | custom-call | tf_op jit(solution)/shard_map/place/pallas_call | solution.py:733
